TPU v7x, 128 devices: a whole 4x4x4 slice. The times are simulated.
128 devices in a mesh: chain: 32 (over x_hi, y, z), group: 4 (over x_lo, core).
Axes of the slice: x: 4 (x_hi: 2, x_lo: 2; x = x_hi * 2 + x_lo), y: 4, z: 4, core: 2. Of those that a mesh axis runs over, the one named last changes fastest.
Arguments:
- site_tensors: bfloat16 [4, 32, 16, 256, 2, 256], P('group', 'chain')
- bond_weights: float32 [4, 32, 16, 256], P('group', 'chain'), may hold values from 0.5 to 1.5
- sector_sizes: int32 [4, 32, 16], P('group', 'chain'), may hold values from 192 to 256, as said below
- kept_ranks: int32 [4, 32, 16], P('group', 'chain'), may hold values from 128 to 256, as said below
- sketches: bfloat16 [16, 512, 256], replicated, may hold values from -6 to 6
- gate_ends: float32 [2], replicated, may hold values from 0.5 to 1.5
- gate_pair: float32 [3], replicated, may hold values from -0.4 to 0.4
Outputs:
- updated_sites: bfloat16 [4, 32, 16, 256, 2, 256], P('group', 'chain')
Inputs may be any that keep to these rules, and one draw needn't show every extreme that they name: `sector_sizes`: every bond has one charge sector, the same for all bonds of a draw, of size 256. `kept_ranks`: A kept rank of sector q of bond n is at most the size of sector q of bonds n - 1, n and n + 1 (bonds outside the MPS count as 256); in the sector of size 256 it equals 256.
All inputs are finite; a program needn't handle non-finite values.
Results may differ from a plain program's by a relative error of at most 0.0088.
Values may be sent and summed in bfloat16 or wider, within the bound.
No kernel may reach another device: no remote copies, remote signals or barrier semaphores. Data moves between devices by JAX's collectives and lax.ppermute only.
A program may use at most 192 MiB of HBM per device.

v0:
```python
import functools

import jax
import jax.numpy as jnp
from jax import lax
from jax.experimental import pallas as pl
from jax.experimental.pallas import tpu as pltpu
from jax.sharding import PartitionSpec as P

f32 = jnp.float32
bf16 = jnp.bfloat16


BATCH = 4
LEAF = 32
PANELS = 8
LANES = 128
SIZE = 256


def split(x):
    high = x.astype(bf16)
    return high, (x - high.astype(f32)).astype(bf16)


def invert_leaf(d):
    lane = lax.broadcasted_iota(jnp.int32, (8, LANES), 1)
    sub = lax.broadcasted_iota(jnp.int32, (8, LANES), 0)
    segment = (lane // LEAF) * LEAF
    tiles = LEAF // 8
    rows = [d[8 * t : 8 * t + 8, :] for t in range(tiles)]
    cols = [
        [
            jnp.take_along_axis(rows[t], segment + j, axis=1) if t >= j // 8 else None
            for t in range(tiles)
        ]
        for j in range(LEAF)
    ]
    inverse = [((lane - segment) == (sub + 8 * t)).astype(f32) for t in range(tiles)]
    pivots = [jnp.ones((8, LANES), f32) for _ in range(tiles)]

    def row(v, r):
        return jnp.broadcast_to(v[r : r + 1, :], (8, LANES))

    for j in range(LEAF):
        top, r = j // 8, j % 8
        pivot = row(cols[j][top], r)
        reciprocal = 1.0 / pivot
        pivots[top] = jnp.where(sub == r, pivot, pivots[top])
        scaled = {t: cols[j][t] * reciprocal for t in range(top, tiles)}
        for i in range(j + 1, LEAF):
            factor = row(scaled[i // 8], i % 8)
            for t in range(i // 8, tiles):
                cols[i][t] = cols[i][t] - factor * cols[j][t]
        source = row(inverse[top], r)
        for t in range(top, tiles):
            factor = jnp.where(sub > r, scaled[t], 0.0) if t == top else scaled[t]
            inverse[t] = inverse[t] - factor * source
    return jnp.concatenate([inverse[t] * lax.rsqrt(pivots[t]) for t in range(tiles)], axis=0)


def block_weights(high, low, masks):
    high = jnp.concatenate([high * mask for mask in masks], axis=0)
    low = jnp.concatenate([low * mask for mask in masks], axis=0)
    upper = jnp.concatenate([high, high], axis=1)
    lower = jnp.concatenate([low, jnp.zeros_like(low)], axis=1)
    return jnp.concatenate([upper, lower], axis=0)


def times_transposed(x, weights):
    out = lax.dot_general(x, weights, (((1,), (1,)), ((), ())), preferred_element_type=f32)
    return out[:, :LANES] + out[:, LANES:]


def invert_factor(a_ref, x_ref):
    lane = lax.broadcasted_iota(jnp.int32, (LEAF, LANES), 1)
    sub = lax.broadcasted_iota(jnp.int32, (LEAF, LANES), 0)
    eye = ((lane % LEAF) == sub).astype(f32)
    masks = [((lane // LEAF) == b).astype(f32).astype(bf16) for b in range(BATCH)]
    for j in range(PANELS):
        start = j * LEAF
        block = slice(start, start + LEAF)
        col = a_ref[j]
        if j:
            weights = [
                block_weights(
                    x_ref[block, k * SIZE : k * SIZE + LANES],
                    x_ref[block, k * SIZE + LANES : (k + 1) * SIZE],
                    masks,
                )
                for k in range(j)
            ]
            col = col - times_transposed(x_ref[:, : j * SIZE], jnp.concatenate(weights, axis=1))
            x_ref[block, : j * SIZE] = jnp.zeros((LEAF, j * SIZE), bf16)
        inverse = invert_leaf(col[block])
        col = jnp.concatenate(
            [part for part in (col[:start], eye, col[start + LEAF :]) if part.shape[0]], axis=0
        )
        col = times_transposed(
            jnp.concatenate(split(col), axis=1), block_weights(*split(inverse), masks)
        )
        x_ref[:, j * SIZE : (j + 1) * SIZE] = jnp.concatenate(split(col), axis=1)


def compute_kernel(second, *refs):
    if second:
        (role, gates, kept, own, got, got_b, half, scale, sketches, carry) = refs[:10]
        (msg, out, merge), refs = refs[11:14], refs[14:]
    else:
        (role, gates, kept, own, got, scale, sketches) = refs[:7]
        (msg, out, carry_out), refs = refs[7:10], refs[10:]
    left_w, right_w, mixed, samp, gram, a_ref, x_ref, scaled_ref, wide_t, wide_p = refs[:10]
    own_win, got_win, sketch, mine, own_sem, got_sem, sketch_sem, mine_sem = refs[10:]
    is_right = role[0] == 1
    first = role[1]
    g0, g1, p0, p1, p2 = [gates[i] for i in range(5)]

    def own_copy(t):
        at = jnp.clip(first - 1 + t, 0, 15)
        return pltpu.make_async_copy(own.at[at], own_win.at[t], own_sem.at[t])

    def got_copy(t, source):
        return pltpu.make_async_copy(source, got_win.at[t], got_sem.at[t])

    if second:
        sources = [None, got_b.at[0], got_b.at[1], got_b.at[2], got.at[0], got.at[1]]
    else:
        sources = [got.at[t] for t in range(5)] + [got.at[0]]
    sketch_copy = pltpu.make_async_copy(sketches.at[pl.ds(first, BATCH)], sketch, sketch_sem)
    for t in range(6):
        own_copy(t).start()
        if sources[t] is not None:
            got_copy(t, sources[t]).start()
    sketch_copy.start()
    if second:
        for jb in range(2):
            wide_t[pl.ds(2 * jb, SIZE, stride=4), :] = jnp.zeros((SIZE, LANES), f32)
            wide_t[pl.ds(2 * jb + 1, SIZE, stride=4), :] = half[
                :, jb * LANES : (jb + 1) * LANES
            ].astype(f32)
        got_win[0] = wide_t[...].astype(bf16)

    def row_scale(which, q):
        line = scale[which, q + 1]
        return jnp.transpose(jnp.broadcast_to(line, (LANES, SIZE)))

    def weigh(t, loop):
        q = first - 1 + t
        own_copy(t).wait()

        @pl.when(t >= (1 if second else 0))
        def _():
            got_copy(t, got.at[0]).wait()

        own_wide = own_win[t].astype(f32)
        got_wide = got_win[t].astype(f32)
        wide_t[...] = jnp.where(is_right, got_wide, own_wide)
        wide_p[...] = jnp.where(is_right, own_wide, got_wide)
        left_rows = row_scale(0, q)
        right_rows = row_scale(1, q)
        for s in range(2):
            col = scale[2, q + s + 1]
            for jb in range(2):
                lines = pl.ds(2 * jb + s, SIZE, stride=4)
                lanes = slice(jb * LANES, (jb + 1) * LANES)
                left_w[t, s, :, lanes] = (wide_t[lines, :] * left_rows).astype(bf16)
                value = (wide_p[lines, :] * right_rows) * col[:, lanes]
                right_w[t, s, :, lanes] = value.astype(bf16)
        return loop

    lax.fori_loop(0, 6, weigh, 0)

    def dot(a, b):
        return jnp.dot(a, b, preferred_element_type=f32)

    lane256 = lax.broadcasted_iota(jnp.int32, (1, SIZE), 1)
    eye = lax.broadcasted_iota(jnp.int32, (SIZE, SIZE), 0) == lax.broadcasted_iota(
        jnp.int32, (SIZE, SIZE), 1
    )
    upper, lower = slice(0, SIZE), slice(SIZE, 2 * SIZE)
    contract_rows = (((0,), (0,)), ((), ()))
    sketch_copy.wait()

    def sample(b, loop):
        t = b + 1
        left = [left_w[t, 0], left_w[t, 1], left_w[b, 0], left_w[b, 1]]
        right = [right_w[t, 0], right_w[t, 1]]
        mixed[b, upper, upper] = (g0 * dot(left[0], right[0])).astype(bf16)
        mixed[b, upper, lower] = (
            p0 * dot(left[0], right[1]) + p2 * dot(left[1], right_w[t + 1, 0])
        ).astype(bf16)
        mixed[b, lower, upper] = (
            p2 * dot(left[2], right_w[b, 1]) + p1 * dot(left[3], right[0])
        ).astype(bf16)
        mixed[b, lower, lower] = (g1 * dot(left[3], right[1])).astype(bf16)
        keep = lane256 < kept[first + b]
        sampled = jnp.where(keep, dot(mixed[b], sketch[b]), 0.0)
        high, low = split(sampled)
        samp[b, 0] = high
        samp[b, 1] = low
        shift = 0.01 * jnp.sum(sampled * sampled) / SIZE
        hh = lax.dot_general(high, high, contract_rows, preferred_element_type=f32)
        hl = lax.dot_general(high, low, contract_rows, preferred_element_type=f32)
        added = jnp.where(keep, 0.0, 1.0) + shift
        gram[b] = (hh + (hl + jnp.transpose(hl))) + jnp.where(eye, added, 0.0)
        return loop

    lax.fori_loop(0, BATCH, sample, 0)

    segment = lax.broadcasted_iota(jnp.int32, (1, LANES), 1) // LEAF

    def gather_lanes(pieces):
        out = pieces[0]
        for i in range(1, BATCH):
            out = jnp.where(segment == i, pieces[i], out)
        return out

    def rolled(value, segments):
        shift = (segments * LEAF) % LANES
        return pltpu.roll(value, shift, axis=1) if shift else value

    for k in range(PANELS):
        rows = slice(k * LEAF, SIZE)
        lanes = slice((k // 4) * LANES, (k // 4 + 1) * LANES)
        a_ref[k, rows, :] = gather_lanes(
            [rolled(gram[b, rows, lanes], b - k % 4) for b in range(BATCH)]
        )
        if k:
            a_ref[k, : k * LEAF, :] = jnp.zeros((k * LEAF, LANES), f32)

    invert_factor(a_ref, x_ref)

    for b in range(BATCH):
        high, low = [
            jnp.concatenate(
                [
                    gather_lanes(
                        [
                            rolled(
                                x_ref[:, k * SIZE + offset : k * SIZE + offset + LANES].astype(f32),
                                k % 4 - b,
                            )
                            for k in range(4 * g, 4 * g + 4)
                        ]
                    )
                    for g in range(2)
                ],
                axis=1,
            ).astype(bf16)
            for offset in (0, LANES)
        ]
        solved = dot(samp[b, 0], high) + (dot(samp[b, 0], low) + dot(samp[b, 1], high))
        scaled_ref[b] = (solved * 16.0).astype(bf16)

    if second:
        scaled_ref[BATCH, lower, :] = carry[...]
    else:
        scaled_ref[BATCH, lower, :] = jnp.zeros((SIZE, SIZE), bf16)
        carry_out[...] = scaled_ref[0, lower, :]

    def deliver(b, loop):
        right_part = lax.dot_general(
            scaled_ref[b], mixed[b], contract_rows, preferred_element_type=f32
        ) * (1.0 / SIZE)
        for s in range(2):
            left_half = scaled_ref[b, upper, :] if s == 0 else scaled_ref[b + 1, lower, :]
            for jb in range(2):
                lines = pl.ds(2 * jb + s, SIZE, stride=4)
                wide_t[lines, :] = left_half[:, jb * LANES : (jb + 1) * LANES].astype(f32)
                start = s * SIZE + jb * LANES
                wide_p[lines, :] = right_part[:, start : start + LANES]
        left_site = wide_t[...]
        right_site = wide_p[...]
        msg[b] = jnp.where(is_right, left_site, right_site).astype(bf16)
        mine[b] = jnp.where(is_right, right_site, left_site).astype(bf16)
        mine_copy(b).start()
        return loop

    def mine_copy(b):
        at = first + b
        return pltpu.make_async_copy(mine.at[b], out.at[at], mine_sem.at[b])

    lax.fori_loop(0, BATCH, deliver, 0)

    if second:
        used = jnp.where(is_right, 0.0, 1.0)
        for jb in range(2):
            value = scaled_ref[0, lower, jb * LANES : (jb + 1) * LANES].astype(f32)
            wide_t[pl.ds(2 * jb, SIZE, stride=4), :] = jnp.zeros((SIZE, LANES), f32)
            wide_t[pl.ds(2 * jb + 1, SIZE, stride=4), :] = value * used
        merge[...] = wide_t[...].astype(bf16)
    for b in range(BATCH):
        mine_copy(b).wait()


def in_hbm(x):
    return pltpu.with_memory_space_constraint(x, pltpu.HBM)


def compute(second, role, gates, kept, own, got, scale, sketch, got_b=None, half=None, carry=None, out=None):
    smem = pl.BlockSpec(memory_space=pltpu.SMEM)
    vmem = pl.BlockSpec(memory_space=pltpu.VMEM)
    hbm = pl.BlockSpec(memory_space=pltpu.HBM)
    own, got, sketch = in_hbm(own), in_hbm(got), in_hbm(sketch)
    if second:
        operands = (role, gates, kept, own, got, in_hbm(got_b), half, scale, sketch, carry, out)
        specs = [smem] * 3 + [hbm] * 3 + [vmem, vmem, hbm, vmem, hbm]
        third = jax.ShapeDtypeStruct((4 * SIZE, LANES), bf16)
    else:
        operands = (role, gates, kept, own, got, scale, sketch)
        specs = [smem] * 3 + [hbm] * 2 + [vmem, hbm]
        third = jax.ShapeDtypeStruct((SIZE, SIZE), bf16)
    part = jax.ShapeDtypeStruct((BATCH, 4 * SIZE, LANES), bf16)
    whole = jax.ShapeDtypeStruct(own.shape, bf16)
    return pl.pallas_call(
        functools.partial(compute_kernel, second),
        out_shape=(part, whole, third),
        in_specs=specs,
        out_specs=(vmem, hbm, vmem),
        scratch_shapes=[
            pltpu.VMEM((6, 2, SIZE, SIZE), bf16),
            pltpu.VMEM((6, 2, SIZE, SIZE), bf16),
            pltpu.VMEM((BATCH, 2 * SIZE, 2 * SIZE), bf16),
            pltpu.VMEM((BATCH, 2, 2 * SIZE, SIZE), bf16),
            pltpu.VMEM((BATCH, SIZE, SIZE), f32),
            pltpu.VMEM((PANELS, SIZE, LANES), f32),
            pltpu.VMEM((SIZE, PANELS * SIZE), bf16),
            pltpu.VMEM((BATCH + 1, 2 * SIZE, SIZE), bf16),
            pltpu.VMEM((4 * SIZE, LANES), f32),
            pltpu.VMEM((4 * SIZE, LANES), f32),
            pltpu.VMEM((6, 4 * SIZE, LANES), bf16),
            pltpu.VMEM((6, 4 * SIZE, LANES), bf16),
            pltpu.VMEM((BATCH, 2 * SIZE, SIZE), bf16),
            pltpu.VMEM((BATCH, 4 * SIZE, LANES), bf16),
            pltpu.SemaphoreType.DMA((6,)),
            pltpu.SemaphoreType.DMA((6,)),
            pltpu.SemaphoreType.DMA,
            pltpu.SemaphoreType.DMA((BATCH,)),
        ],
        input_output_aliases={10: 1} if second else {},
        compiler_params=pltpu.CompilerParams(vmem_limit_bytes=40 * 2**20),
        cost_estimate=pl.CostEstimate(
            flops=20_000_000_000, bytes_accessed=8_000_000, transcendentals=0
        ),
        name="second_half" if second else "first_half",
    )(*operands)


def place_kernel(merged, at, block, *refs):
    if merged:
        merge, _, out, last, sems = refs
    else:
        _, out, sems = refs
    count = block.shape[0]
    copies = []
    for b in range(count):
        source = block.at[b]
        if merged and b == count - 1:
            last[...] = block[b] + merge[...]
            source = last
        copies.append(pltpu.make_async_copy(source, out.at[at[0] + b], sems.at[b]))
        copies[-1].start()
    for copy in copies:
        copy.wait()


def place(out, block, at, merge=None):
    smem = pl.BlockSpec(memory_space=pltpu.SMEM)
    vmem = pl.BlockSpec(memory_space=pltpu.VMEM)
    hbm = pl.BlockSpec(memory_space=pltpu.HBM)
    operands = (jnp.reshape(at, (1,)), block) + (() if merge is None else (merge,)) + (out,)
    scratch = [] if merge is None else [pltpu.VMEM(merge.shape, bf16)]
    return pl.pallas_call(
        functools.partial(place_kernel, merge is not None),
        out_shape=jax.ShapeDtypeStruct(out.shape, out.dtype),
        in_specs=[smem] + [vmem] * (len(operands) - 2) + [hbm],
        out_specs=hbm,
        scratch_shapes=scratch + [pltpu.SemaphoreType.DMA((block.shape[0],))],
        input_output_aliases={len(operands) - 1: 0},
        compiler_params=pltpu.CompilerParams(vmem_limit_bytes=8 * 2**20),
        cost_estimate=pl.CostEstimate(flops=1000000, bytes_accessed=2_000_000, transcendentals=0),
        name="place",
    )(*operands)


def to_lines(x):
    n = x.shape[0]
    return x.reshape(n, SIZE, 2, 2, LANES).transpose(0, 1, 3, 2, 4).reshape(n, 4 * SIZE, LANES)


def from_lines(x):
    n = x.shape[0]
    return x.reshape(n, SIZE, 2, 2, LANES).transpose(0, 1, 3, 2, 4).reshape(n, SIZE, 2, SIZE)


def shards(site_tensors, bond_weights, sector_sizes, kept_ranks, sketches, gate_ends, gate_pair):
    chain = lax.axis_size("chain")
    count = lax.axis_size("group") * chain
    site = lax.axis_index("group") * chain + lax.axis_index("chain")
    is_right = site % 2 == 1

    def swapped(value):
        return lax.ppermute(value, "chain", [(i, i ^ 1) for i in range(chain)])

    def onward(value, by):
        def place(n):
            return n % chain * (count // chain) + n // chain

        pairs = [(place(i), place(i + by)) for i in range(1, count, 2) if i + by < count]
        return lax.ppermute(value, ("chain", "group"), pairs)

    own = to_lines(site_tensors[0, 0])
    sectors = own.shape[0]
    got_a = swapped(lax.dynamic_slice_in_dim(own, jnp.where(is_right, 11, 3), 5, 0))

    column = lax.broadcasted_iota(jnp.int32, (sectors, SIZE), 1)
    lam = bond_weights[0, 0] * (column < sector_sizes[0, 0][:, None]).astype(f32)
    kept_line = jnp.pad(kept_ranks[0, 0].astype(f32)[None, :], ((0, 7), (0, SIZE - sectors)))
    packed = jnp.concatenate([lam, kept_line], axis=0)
    other = swapped(packed)
    before_left = onward(lam, 1)
    before_right = onward(lam, 2)

    got_b = swapped(lax.dynamic_slice_in_dim(own, jnp.where(is_right, 8, 0), 3, 0))
    half = lax.ppermute(
        site_tensors[0, 0, 7, :, 1, :], "chain", [(i, i - 1) for i in range(1, chain, 2)]
    )

    lam_prev = jnp.where(is_right, before_right, before_left)
    lam_prev = jnp.where(site < 2, jnp.ones_like(lam), lam_prev)
    lam_mid = jnp.where(is_right, other[:sectors], lam)
    lam_next = jnp.where(is_right, lam, other[:sectors])
    scale = jnp.pad(jnp.stack([lam_prev, lam_mid, lam_next]), ((0, 0), (1, 7), (0, 0)))
    scale = scale[:, :, None, :]
    kept = jnp.where(is_right, other[sectors, :sectors], kept_line[0, :sectors]).astype(jnp.int32)
    gates = jnp.concatenate([gate_ends, 1.0 + gate_pair[:2], gate_pair[2:]])
    flag = is_right.astype(jnp.int32)
    role_a = jnp.stack([flag, 12 - 8 * flag])
    role_b = jnp.stack([flag, 8 - 8 * flag])

    msg_a, out, carry = compute(False, role_a, gates, kept, own, got_a, scale, sketches)
    back_a = swapped(msg_a)
    msg_b, out, merge = compute(
        True, role_b, gates, kept, own, got_a, scale, sketches, got_b, half, carry, out
    )
    back_b = swapped(msg_b)

    back_at = 8 * flag
    out = place(out, back_a, back_at + 4, merge)
    out = place(out, back_b, back_at)
    return from_lines(out)[None, None]


def solution(mesh):
    return jax.shard_map(
        shards,
        mesh=mesh,
        in_specs=(
            P("group", "chain", None, None, None, None),
            P("group", "chain", None, None),
            P("group", "chain", None),
            P("group", "chain", None),
            P(),
            P(),
            P(),
        ),
        out_specs=P("group", "chain", None, None, None, None),
        check_vma=False,
    )
```

profile of v0, /device:TPU:0, one launch (start us, length us, event | category | flops | bytes accessed | tf_op | source)
XLA Modules:
  0.0 108.4 jit_solution(8071605048716240867)
XLA Ops:
  0.0 0.0 copy-start.1
  0.0 0.0 copy-start
  0.0 0.0 copy-start.3
  0.0 0.0 copy-start.4
  0.0 0.0 copy-start.2
  0.0 0.9 bitcast_select_fusion
  0.9 0.7 collective-permute-start.4
  1.5 0.7 collective-permute-start.5
  2.2 1.4 %constant_dynamic-slice_fusion.1 = bf16[5,1024,128]{2,1,0:T(8,128)(2,1)S(1)} fusion(bf16[16,1024,128]{2,1,0:T(8,128)(2,1)} %bitcast.37, s32[]{:T(128)S(6)} %select_n.47), kind=kLoop, calls=%fused_computation.22 | loop fusion | bytes 2621444 | tf_op jit(solution)/shard_map/dynamic_slice | solution.py:414
  3.6 7.0 %collective-permute-start.1 = (bf16[5,1024,128]{2,1,0:T(8,128)(2,1)S(1)}, bf16[5,1024,128]{2,1,0:T(8,128)(2,1)}, u32[]{:S(2)}, u32[]{:S(2)}) collective-permute-start(bf16[5,1024,128]{2,1,0:T(8,128)(2,1)S(1)} %constant_dynamic-slice_fusion.1), channel_id=1, source_target_pairs={{0,4},{4,0},{8,12},{12,8},{16,20},{20,16},{24,28},{28,24},{32,36},... | collective-permute-start | bytes 3932168 | tf_op jit(solution)/shard_map/ppermute | solution.py:403
  10.6 0.7 convert_bitcast_fusion
  11.2 0.0 collective-permute-start
  11.3 1.2 %constant_dynamic-slice_fusion = bf16[3,1024,128]{2,1,0:T(8,128)(2,1)S(1)} fusion(bf16[16,1024,128]{2,1,0:T(8,128)(2,1)} %bitcast.38, s32[]{:T(128)} %mul.12), kind=kLoop, calls=%fused_computation.21 | loop fusion | bytes 1572868 | tf_op jit(solution)/shard_map/dynamic_slice | solution.py:424
  12.5 2.1 %collective-permute-start.2 = (bf16[3,1024,128]{2,1,0:T(8,128)(2,1)S(1)}, bf16[3,1024,128]{2,1,0:T(8,128)(2,1)}, u32[]{:S(2)}, u32[]{:S(2)}) collective-permute-start(bf16[3,1024,128]{2,1,0:T(8,128)(2,1)S(1)} %constant_dynamic-slice_fusion), channel_id=1, source_target_pairs={{0,4},{4,0},{8,12},{12,8},{16,20},{20,16},{24,28},{28,24},{32,36},... | collective-permute-start | bytes 2359304 | tf_op jit(solution)/shard_map/ppermute | solution.py:403
  14.5 0.0 copy-done.4
  14.5 0.6 slice.18
  15.2 0.1 pad_add_fusion.1.refs_0_
  15.3 0.1 pad_add_fusion.refs_0_
  15.3 0.0 copy-done.2
  15.4 0.7 pad_maximum_fusion.refs_1_
  16.1 1.2 %slice.20 = bf16[1,1,1,256,1,256]{5,4,3,2,1,0:T(2,128)(2,1)S(1)} slice(bf16[1,1,16,256,2,256]{5,4,3,2,1,0:T(2,128)(2,1)} %param.7), slice={[0:1], [0:1], [7:8], [0:256], [1:2], [0:256]} | slice | bytes 262144 | tf_op jit(solution)/shard_map/slice | solution.py:426
  17.3 0.0 collective-permute-done.4
  17.3 1.3 %collective-permute-start.3 = (bf16[256,256]{1,0:T(8,128)(2,1)S(1)}, bf16[256,256]{1,0:T(8,128)(2,1)S(1)}, u32[]{:S(2)}, u32[]{:S(2)}) collective-permute-start(bf16[256,256]{1,0:T(8,128)(2,1)S(1)} %bitcast.41), channel_id=1, source_target_pairs={{4,0},{12,8},{20,16},{28,24},{36,32},{44,40},{52,48},{60,56},{68,6... | collective-permute-start | bytes 393224 | tf_op jit(solution)/shard_map/ppermute | solution.py:425
  18.6 0.0 collective-permute-done.5
  18.7 22.1 %collective-permute-done = f32[24,256]{1,0:T(8,128)S(1)} collective-permute-done((f32[24,256]{1,0:T(8,128)S(1)}, f32[24,256]{1,0:T(8,128)S(1)}, u32[]{:S(2)}, u32[]{:S(2)}) %collective-permute-start) | collective-permute-done | bytes 24608 | tf_op jit(solution)/shard_map/ppermute | solution.py:403
  40.7 0.0 copy-done.1
  40.7 0.0 copy-done
  40.7 0.1 select_bitcast_fusion.1
  40.8 0.1 broadcast_in_dim.8.refs_5_.refs_7_
  40.9 0.0 copy-done.3
  40.9 0.0 collective-permute-done.1.refs_4_
  40.9 20.3 %first_half.1 = (bf16[4,1024,128]{2,1,0:T(8,128)(2,1)S(1)}, bf16[16,1024,128]{2,1,0:T(8,128)(2,1)}, bf16[256,256]{1,0:T(8,128)(2,1)S(1)}) custom-call(s32[2]{0:T(128)S(1)} %pad_add_fusion.1.refs_0_, f32[5]{0:T(128)S(1)} %pad_maximum_fusion.refs_1_, s32[16]{0:T(128)S(1)} %fusion.1.refs_2_, bf16[16,1024,128]{2,1,0:T(8,128)(2,1)} %bitcast.39, ...), custom_call_target="tpu_custom_call" | custom-call | flops 20000000000 | bytes 8000000 | tf_op jit(solution)/shard_map/first_half/pallas_call | solution.py:315
  61.2 2.3 %collective-permute-start.7 = (bf16[4,1024,128]{2,1,0:T(8,128)(2,1)S(1)}, bf16[4,1024,128]{2,1,0:T(8,128)(2,1)S(1)}, u32[]{:S(2)}, u32[]{:S(2)}) collective-permute-start(bf16[4,1024,128]{2,1,0:T(8,128)(2,1)S(1)} %get-tuple-element.14), channel_id=1, source_target_pairs={{0,4},{4,0},{8,12},{12,8},{16,20},{20,16},{24,28},{28,24},{32,36},... | collective-permute-start | bytes 3145736 | tf_op jit(solution)/shard_map/ppermute | solution.py:403
  63.5 0.0 collective-permute-done.3.refs_6_
  63.5 0.0 collective-permute-done.2.refs_5_
  63.5 21.3 %second_half.1 = (bf16[4,1024,128]{2,1,0:T(8,128)(2,1)}, bf16[16,1024,128]{2,1,0:T(8,128)(2,1)}, bf16[1024,128]{1,0:T(8,128)(2,1)S(1)}) custom-call(s32[2]{0:T(128)S(1)} %pad_add_fusion.refs_0_, f32[5]{0:T(128)S(1)} %pad_maximum_fusion.refs_1_, s32[16]{0:T(128)S(1)} %fusion.1.refs_2_, ...), custom_call_target="tpu_custom_call", output_to_operand_aliasing={{1}: (10, {})} | custom-call | flops 20000000000 | bytes 8000000 | tf_op jit(solution)/shard_map/second_half/pallas_call | solution.py:315
  84.8 0.1 collective-permute-start.6
  84.9 0.0 collective-permute-done.7.block
  84.9 1.0 place.2.refs_0_
  85.9 21.3 %collective-permute-done.6.block = bf16[4,1024,128]{2,1,0:T(8,128)(2,1)S(1)} collective-permute-done((bf16[4,1024,128]{2,1,0:T(8,128)(2,1)}, bf16[4,1024,128]{2,1,0:T(8,128)(2,1)S(1)}, u32[]{:S(2)}, u32[]{:S(2)}) %collective-permute-start.6) | collective-permute-done | bytes 1048608 | tf_op jit(solution)/shard_map/ppermute | solution.py:403
  107.3 1.0 place.3
  (6 shorter events, 0.1 us)
Async XLA Ops:
  0.0 40.7 %copy-start.1 = (s32[1,1,16]{2,1,0:T(1,128)S(1)}, s32[1,1,16]{2,1,0:T(1,128)}, u32[]{:S(2)}) copy-start(s32[1,1,16]{2,1,0:T(1,128)} %param.9) | copy-start | bytes 196
  0.0 40.7 %copy-start = (f32[1,1,16,256]{3,2,1,0:T(8,128)S(1)}, f32[1,1,16,256]{3,2,1,0:T(8,128)}, u32[]{:S(2)}) copy-start(f32[1,1,16,256]{3,2,1,0:T(8,128)} %param.8) | copy-start | bytes 49156
  0.0 40.9 %copy-start.3 = (s32[1,1,16]{2,1,0:T(1,128)S(1)}, s32[1,1,16]{2,1,0:T(1,128)}, u32[]{:S(2)}) copy-start(s32[1,1,16]{2,1,0:T(1,128)} %param.10) | copy-start | bytes 196
  0.0 14.5 %copy-start.4 = (f32[3]{0:T(128)S(1)}, f32[3]{0:T(128)}, u32[]{:S(2)}) copy-start(f32[3]{0:T(128)} %param.13) | copy-start | bytes 40
  0.0 15.3 %copy-start.2 = (f32[2]{0:T(128)S(1)}, f32[2]{0:T(128)}, u32[]{:S(2)}) copy-start(f32[2]{0:T(128)} %param.12) | copy-start | bytes 28
  0.9 16.5 %collective-permute-start.4 = (f32[16,256]{1,0:T(8,128)S(1)}, f32[16,256]{1,0:T(8,128)S(1)}, u32[]{:S(2)}, u32[]{:S(2)}) collective-permute-start(f32[16,256]{1,0:T(8,128)S(1)} %bitcast_select_fusion), channel_id=1, source_target_pairs={{4,12},{12,20},{20,28},{28,36},{36,44},{44,52},{52,60},{60,68},{68... | collective-permute-start | bytes 49160 | tf_op jit(solution)/shard_map/ppermute | solution.py:410
  1.5 17.1 %collective-permute-start.5 = (f32[16,256]{1,0:T(8,128)S(1)}, f32[16,256]{1,0:T(8,128)S(1)}, u32[]{:S(2)}, u32[]{:S(2)}) collective-permute-start(f32[16,256]{1,0:T(8,128)S(1)} %bitcast_select_fusion), channel_id=1, source_target_pairs={{4,8},{12,16},{20,24},{28,32},{36,40},{44,48},{52,56},{60,64},{68,... | collective-permute-start | bytes 49160 | tf_op jit(solution)/shard_map/ppermute | solution.py:410
  3.6 37.3 %collective-permute-start.1 = (bf16[5,1024,128]{2,1,0:T(8,128)(2,1)S(1)}, bf16[5,1024,128]{2,1,0:T(8,128)(2,1)}, u32[]{:S(2)}, u32[]{:S(2)}) collective-permute-start(bf16[5,1024,128]{2,1,0:T(8,128)(2,1)S(1)} %constant_dynamic-slice_fusion.1), channel_id=1, source_target_pairs={{0,4},{4,0},{8,12},{12,8},{16,20},{20,16},{24,28},{28,24},{32,36},... | collective-permute-start | bytes 3932168 | tf_op jit(solution)/shard_map/ppermute | solution.py:403
  11.2 29.5 %collective-permute-start = (f32[24,256]{1,0:T(8,128)S(1)}, f32[24,256]{1,0:T(8,128)S(1)}, u32[]{:S(2)}, u32[]{:S(2)}) collective-permute-start(f32[24,256]{1,0:T(8,128)S(1)} %select_maximum_fusion.2), channel_id=1, source_target_pairs={{0,4},{4,0},{8,12},{12,8},{16,20},{20,16},{24,28},{28,24},{32,36},... | collective-permute-start | bytes 73736 | tf_op jit(solution)/shard_map/ppermute | solution.py:403
  12.5 51.1 %collective-permute-start.2 = (bf16[3,1024,128]{2,1,0:T(8,128)(2,1)S(1)}, bf16[3,1024,128]{2,1,0:T(8,128)(2,1)}, u32[]{:S(2)}, u32[]{:S(2)}) collective-permute-start(bf16[3,1024,128]{2,1,0:T(8,128)(2,1)S(1)} %constant_dynamic-slice_fusion), channel_id=1, source_target_pairs={{0,4},{4,0},{8,12},{12,8},{16,20},{20,16},{24,28},{28,24},{32,36},... | collective-permute-start | bytes 2359304 | tf_op jit(solution)/shard_map/ppermute | solution.py:403
  17.3 46.2 %collective-permute-start.3 = (bf16[256,256]{1,0:T(8,128)(2,1)S(1)}, bf16[256,256]{1,0:T(8,128)(2,1)S(1)}, u32[]{:S(2)}, u32[]{:S(2)}) collective-permute-start(bf16[256,256]{1,0:T(8,128)(2,1)S(1)} %bitcast.41), channel_id=1, source_target_pairs={{4,0},{12,8},{20,16},{28,24},{36,32},{44,40},{52,48},{60,56},{68,6... | collective-permute-start | bytes 393224 | tf_op jit(solution)/shard_map/ppermute | solution.py:425
  61.2 23.7 %collective-permute-start.7 = (bf16[4,1024,128]{2,1,0:T(8,128)(2,1)S(1)}, bf16[4,1024,128]{2,1,0:T(8,128)(2,1)S(1)}, u32[]{:S(2)}, u32[]{:S(2)}) collective-permute-start(bf16[4,1024,128]{2,1,0:T(8,128)(2,1)S(1)} %get-tuple-element.14), channel_id=1, source_target_pairs={{0,4},{4,0},{8,12},{12,8},{16,20},{20,16},{24,28},{28,24},{32,36},... | collective-permute-start | bytes 3145736 | tf_op jit(solution)/shard_map/ppermute | solution.py:403
  84.8 22.5 %collective-permute-start.6 = (bf16[4,1024,128]{2,1,0:T(8,128)(2,1)}, bf16[4,1024,128]{2,1,0:T(8,128)(2,1)S(1)}, u32[]{:S(2)}, u32[]{:S(2)}) collective-permute-start(bf16[4,1024,128]{2,1,0:T(8,128)(2,1)} %get-tuple-element.13), channel_id=1, source_target_pairs={{0,4},{4,0},{8,12},{12,8},{16,20},{20,16},{24,28},{28,24},{32,36},... | collective-permute-start | bytes 3145736 | tf_op jit(solution)/shard_map/ppermute | solution.py:403
where the time goes:
time: 109 us; the launch traced here: 108 us
  Pallas kernels  43.5 us (40%)
  waiting for transfers between devices  43.4 us (40%)
  starting transfers between devices  14.1 us (13%)
  local copies, waits for them, and re-layouts  4.57 us (4%)
  other arithmetic  2.49 us (2%)
    ppermute x5, waiting for transfers between devices, swapped(): return lax.ppermute(value, 'chain', [(i, i ^ 1) for i in range(chain)])  43.4 us
    pallas_call x2, Pallas kernels, compute(): pl.pallas_call(functools.partial(compute_kernel, second), out_shape=(part...  41.6 us
    ppermute x5, starting transfers between devices, swapped(): return lax.ppermute(value, 'chain', [(i, i ^ 1) for i in range(chain)])  11.5 us
  transfers between devices with their start and end apart: 8, of which 2 were waited for; matrix products, arithmetic and copies ran while one was open for 6% of the time, Pallas kernels for 39%

commit v1 on v0

--- a/solution.py
+++ b/solution.py
@@ -77,21 +77,36 @@
     sub = lax.broadcasted_iota(jnp.int32, (LEAF, LANES), 0)
     eye = ((lane % LEAF) == sub).astype(f32)
     masks = [((lane // LEAF) == b).astype(f32).astype(bf16) for b in range(BATCH)]
+
+    def weights_of(rows, ks):
+        return jnp.concatenate(
+            [
+                block_weights(
+                    x_ref[rows, k * SIZE : k * SIZE + LANES],
+                    x_ref[rows, k * SIZE + LANES : (k + 1) * SIZE],
+                    masks,
+                )
+                for k in ks
+            ],
+            axis=1,
+        )
+
+    partial = None
     for j in range(PANELS):
         start = j * LEAF
         block = slice(start, start + LEAF)
         col = a_ref[j]
         if j:
-            weights = [
-                block_weights(
-                    x_ref[block, k * SIZE : k * SIZE + LANES],
-                    x_ref[block, k * SIZE + LANES : (k + 1) * SIZE],
-                    masks,
+            last = slice((j - 1) * SIZE, j * SIZE)
+            if partial is not None:
+                col = col - partial
+            col = col - times_transposed(x_ref[:, last], weights_of(block, [j - 1]))
+            x_ref[block, : j * SIZE] = jnp.zeros((LEAF, j * SIZE), bf16)
+            if j < PANELS - 1:
+                following = slice(start + LEAF, start + 2 * LEAF)
+                partial = times_transposed(
+                    x_ref[:, : j * SIZE], weights_of(following, range(j))
                 )
-                for k in range(j)
-            ]
-            col = col - times_transposed(x_ref[:, : j * SIZE], jnp.concatenate(weights, axis=1))
-            x_ref[block, : j * SIZE] = jnp.zeros((LEAF, j * SIZE), bf16)
         inverse = invert_leaf(col[block])
         col = jnp.concatenate(
             [part for part in (col[:start], eye, col[start + LEAF :]) if part.shape[0]], axis=0
@@ -103,42 +118,24 @@
 
 
 def compute_kernel(second, *refs):
+    (role, gates, kept, own, got, scale, sketch), refs = refs[:7], refs[7:]
     if second:
-        (role, gates, kept, own, got, got_b, half, scale, sketches, carry) = refs[:10]
-        (msg, out, merge), refs = refs[11:14], refs[14:]
+        carry = refs[0]
+        (msg, out, merge), refs = refs[2:5], refs[5:]
     else:
-        (role, gates, kept, own, got, scale, sketches) = refs[:7]
-        (msg, out, carry_out), refs = refs[7:10], refs[10:]
+        (msg, out, carry), refs = refs[:3], refs[3:]
     left_w, right_w, mixed, samp, gram, a_ref, x_ref, scaled_ref, wide_t, wide_p = refs[:10]
-    own_win, got_win, sketch, mine, own_sem, got_sem, sketch_sem, mine_sem = refs[10:]
+    got_win, mine, got_sem, mine_sem = refs[10:]
     is_right = role[0] == 1
     first = role[1]
+    own_first = role[2]
     g0, g1, p0, p1, p2 = [gates[i] for i in range(5)]
 
-    def own_copy(t):
-        at = jnp.clip(first - 1 + t, 0, 15)
-        return pltpu.make_async_copy(own.at[at], own_win.at[t], own_sem.at[t])
-
-    def got_copy(t, source):
-        return pltpu.make_async_copy(source, got_win.at[t], got_sem.at[t])
-
-    if second:
-        sources = [None, got_b.at[0], got_b.at[1], got_b.at[2], got.at[0], got.at[1]]
-    else:
-        sources = [got.at[t] for t in range(5)] + [got.at[0]]
-    sketch_copy = pltpu.make_async_copy(sketches.at[pl.ds(first, BATCH)], sketch, sketch_sem)
-    for t in range(6):
-        own_copy(t).start()
-        if sources[t] is not None:
-            got_copy(t, sources[t]).start()
-    sketch_copy.start()
-    if second:
-        for jb in range(2):
-            wide_t[pl.ds(2 * jb, SIZE, stride=4), :] = jnp.zeros((SIZE, LANES), f32)
-            wide_t[pl.ds(2 * jb + 1, SIZE, stride=4), :] = half[
-                :, jb * LANES : (jb + 1) * LANES
-            ].astype(f32)
-        got_win[0] = wide_t[...].astype(bf16)
+    def got_copy(t):
+        return pltpu.make_async_copy(got.at[t], got_win.at[t], got_sem.at[t])
+
+    for t in range(got.shape[0]):
+        got_copy(t).start()
 
     def row_scale(which, q):
         line = scale[which, q + 1]
@@ -146,14 +143,16 @@
 
     def weigh(t, loop):
         q = first - 1 + t
-        own_copy(t).wait()
-
-        @pl.when(t >= (1 if second else 0))
-        def _():
-            got_copy(t, got.at[0]).wait()
-
-        own_wide = own_win[t].astype(f32)
-        got_wide = got_win[t].astype(f32)
+        at = jnp.maximum(t - 1, 0) if second else jnp.minimum(t, 4)
+
+        if not (second and isinstance(t, int)):
+
+            @pl.when(True if second else t < 5)
+            def _():
+                got_copy(at).wait()
+
+        own_wide = own[jnp.clip(q, 0, 15) - own_first].astype(f32)
+        got_wide = got_win[at].astype(f32)
         wide_t[...] = jnp.where(is_right, got_wide, own_wide)
         wide_p[...] = jnp.where(is_right, own_wide, got_wide)
         left_rows = row_scale(0, q)
@@ -168,7 +167,28 @@
                 right_w[t, s, :, lanes] = value.astype(bf16)
         return loop
 
-    lax.fori_loop(0, 6, weigh, 0)
+    if second:
+        lax.fori_loop(1, 4, weigh, 0)
+        weigh(0, 0)
+        right_w[0, 1] = carry[6]
+        for s in range(2):
+            left_w[4, s] = carry[1 + s]
+            right_w[4, s] = carry[3 + s]
+        right_w[5, 0] = carry[5]
+    else:
+        lax.fori_loop(0, 6, weigh, 0)
+        for s in range(2):
+            carry[1 + s] = left_w[0, s]
+            carry[3 + s] = right_w[0, s]
+        carry[5] = right_w[1, 0]
+        q = first - 5
+        wide_p[...] = got_win[4].astype(f32)
+        right_rows = row_scale(1, q)
+        col = scale[2, q + 2]
+        for jb in range(2):
+            lanes = slice(jb * LANES, (jb + 1) * LANES)
+            value = (wide_p[pl.ds(2 * jb + 1, SIZE, stride=4), :] * right_rows) * col[:, lanes]
+            carry[6, :, lanes] = value.astype(bf16)
 
     def dot(a, b):
         return jnp.dot(a, b, preferred_element_type=f32)
@@ -179,7 +199,6 @@
     )
     upper, lower = slice(0, SIZE), slice(SIZE, 2 * SIZE)
     contract_rows = (((0,), (0,)), ((), ()))
-    sketch_copy.wait()
 
     def sample(b, loop):
         t = b + 1
@@ -205,7 +224,7 @@
         gram[b] = (hh + (hl + jnp.transpose(hl))) + jnp.where(eye, added, 0.0)
         return loop
 
-    lax.fori_loop(0, BATCH, sample, 0)
+    lax.fori_loop(0, BATCH, sample, 0, unroll=True)
 
     segment = lax.broadcasted_iota(jnp.int32, (1, LANES), 1) // LEAF
 
@@ -253,10 +272,10 @@
         scaled_ref[b] = (solved * 16.0).astype(bf16)
 
     if second:
-        scaled_ref[BATCH, lower, :] = carry[...]
+        scaled_ref[BATCH, lower, :] = carry[0]
     else:
         scaled_ref[BATCH, lower, :] = jnp.zeros((SIZE, SIZE), bf16)
-        carry_out[...] = scaled_ref[0, lower, :]
+        carry[0] = scaled_ref[0, lower, :]
 
     def deliver(b, loop):
         right_part = lax.dot_general(
@@ -280,7 +299,7 @@
         at = first + b
         return pltpu.make_async_copy(mine.at[b], out.at[at], mine_sem.at[b])
 
-    lax.fori_loop(0, BATCH, deliver, 0)
+    lax.fori_loop(0, BATCH, deliver, 0, unroll=True)
 
     if second:
         used = jnp.where(is_right, 0.0, 1.0)
@@ -297,21 +316,54 @@
     return pltpu.with_memory_space_constraint(x, pltpu.HBM)
 
 
-def compute(second, role, gates, kept, own, got, scale, sketch, got_b=None, half=None, carry=None, out=None):
+def pack_kernel(role, own, out, both, sems):
+    flag = role[0]
+    bulk = pltpu.make_async_copy(own.at[pl.ds(3 + 8 * flag, 4)], out.at[pl.ds(0, 4)], sems.at[0])
+    even = pltpu.make_async_copy(own.at[7 + 8 * flag], both.at[0], sems.at[1])
+    odd = pltpu.make_async_copy(own.at[7], both.at[1], sems.at[2])
+    even.start()
+    odd.start()
+    bulk.start()
+    even.wait()
+    odd.wait()
+    is_odd = lax.broadcasted_iota(jnp.int32, (4 * SIZE, LANES), 0) % 2 == 1
+    out[4] = jnp.where(is_odd, both[1].astype(f32), both[0].astype(f32)).astype(bf16)
+    bulk.wait()
+
+
+def pack(role, own):
+    return pl.pallas_call(
+        pack_kernel,
+        out_shape=jax.ShapeDtypeStruct((5,) + own.shape[1:], bf16),
+        in_specs=[
+            pl.BlockSpec(memory_space=pltpu.SMEM),
+            pl.BlockSpec(memory_space=pltpu.HBM),
+        ],
+        out_specs=pl.BlockSpec(memory_space=pltpu.VMEM),
+        scratch_shapes=[
+            pltpu.VMEM((2,) + own.shape[1:], bf16),
+            pltpu.SemaphoreType.DMA((3,)),
+        ],
+        compiler_params=pltpu.CompilerParams(vmem_limit_bytes=4 * 2**20),
+        name="pack",
+    )(role, in_hbm(own))
+
+
+def compute(second, role, gates, kept, own, got, scale, sketch, carry=None, out=None):
     smem = pl.BlockSpec(memory_space=pltpu.SMEM)
     vmem = pl.BlockSpec(memory_space=pltpu.VMEM)
     hbm = pl.BlockSpec(memory_space=pltpu.HBM)
-    own, got, sketch = in_hbm(own), in_hbm(got), in_hbm(sketch)
+    operands = (role, gates, kept, own, in_hbm(got), scale, sketch)
+    specs = [smem] * 3 + [vmem, hbm, vmem, vmem]
     if second:
-        operands = (role, gates, kept, own, got, in_hbm(got_b), half, scale, sketch, carry, out)
-        specs = [smem] * 3 + [hbm] * 3 + [vmem, vmem, hbm, vmem, hbm]
+        operands += (carry, out)
+        specs += [vmem, hbm]
         third = jax.ShapeDtypeStruct((4 * SIZE, LANES), bf16)
+        whole = jax.ShapeDtypeStruct(out.shape, bf16)
     else:
-        operands = (role, gates, kept, own, got, scale, sketch)
-        specs = [smem] * 3 + [hbm] * 2 + [vmem, hbm]
-        third = jax.ShapeDtypeStruct((SIZE, SIZE), bf16)
+        third = jax.ShapeDtypeStruct((7, SIZE, SIZE), bf16)
+        whole = jax.ShapeDtypeStruct((16, 4 * SIZE, LANES), bf16)
     part = jax.ShapeDtypeStruct((BATCH, 4 * SIZE, LANES), bf16)
-    whole = jax.ShapeDtypeStruct(own.shape, bf16)
     return pl.pallas_call(
         functools.partial(compute_kernel, second),
         out_shape=(part, whole, third),
@@ -328,17 +380,13 @@
             pltpu.VMEM((BATCH + 1, 2 * SIZE, SIZE), bf16),
             pltpu.VMEM((4 * SIZE, LANES), f32),
             pltpu.VMEM((4 * SIZE, LANES), f32),
-            pltpu.VMEM((6, 4 * SIZE, LANES), bf16),
-            pltpu.VMEM((6, 4 * SIZE, LANES), bf16),
-            pltpu.VMEM((BATCH, 2 * SIZE, SIZE), bf16),
+            pltpu.VMEM(got.shape, bf16),
             pltpu.VMEM((BATCH, 4 * SIZE, LANES), bf16),
-            pltpu.SemaphoreType.DMA((6,)),
-            pltpu.SemaphoreType.DMA((6,)),
-            pltpu.SemaphoreType.DMA,
+            pltpu.SemaphoreType.DMA((got.shape[0],)),
             pltpu.SemaphoreType.DMA((BATCH,)),
         ],
-        input_output_aliases={10: 1} if second else {},
-        compiler_params=pltpu.CompilerParams(vmem_limit_bytes=40 * 2**20),
+        input_output_aliases={8: 1} if second else {},
+        compiler_params=pltpu.CompilerParams(vmem_limit_bytes=22 * 2**20),
         cost_estimate=pl.CostEstimate(
             flops=20_000_000_000, bytes_accessed=8_000_000, transcendentals=0
         ),
@@ -411,7 +459,12 @@
 
     own = to_lines(site_tensors[0, 0])
     sectors = own.shape[0]
-    got_a = swapped(lax.dynamic_slice_in_dim(own, jnp.where(is_right, 11, 3), 5, 0))
+    flag = is_right.astype(jnp.int32)
+
+    def window(array, start, size):
+        return lax.dynamic_slice_in_dim(array, start, size, 0)
+
+    got_a = swapped(pack(jnp.reshape(flag, (1,)), own))
 
     column = lax.broadcasted_iota(jnp.int32, (sectors, SIZE), 1)
     lam = bond_weights[0, 0] * (column < sector_sizes[0, 0][:, None]).astype(f32)
@@ -421,10 +474,7 @@
     before_left = onward(lam, 1)
     before_right = onward(lam, 2)
 
-    got_b = swapped(lax.dynamic_slice_in_dim(own, jnp.where(is_right, 8, 0), 3, 0))
-    half = lax.ppermute(
-        site_tensors[0, 0, 7, :, 1, :], "chain", [(i, i - 1) for i in range(1, chain, 2)]
-    )
+    got_b = swapped(window(own, 8 * flag, 3))
 
     lam_prev = jnp.where(is_right, before_right, before_left)
     lam_prev = jnp.where(site < 2, jnp.ones_like(lam), lam_prev)
@@ -434,14 +484,28 @@
     scale = scale[:, :, None, :]
     kept = jnp.where(is_right, other[sectors, :sectors], kept_line[0, :sectors]).astype(jnp.int32)
     gates = jnp.concatenate([gate_ends, 1.0 + gate_pair[:2], gate_pair[2:]])
-    flag = is_right.astype(jnp.int32)
-    role_a = jnp.stack([flag, 12 - 8 * flag])
-    role_b = jnp.stack([flag, 8 - 8 * flag])
-
-    msg_a, out, carry = compute(False, role_a, gates, kept, own, got_a, scale, sketches)
+    first_a = 12 - 8 * flag
+    first_b = 8 - 8 * flag
+    own_a = 10 - 7 * flag
+    own_b = 7 - 7 * flag
+    role_a = jnp.stack([flag, first_a, own_a])
+    role_b = jnp.stack([flag, first_b, own_b])
+
+    msg_a, out, carry = compute(
+        False, role_a, gates, kept, window(own, own_a, 6), got_a, scale, window(sketches, first_a, 4)
+    )
     back_a = swapped(msg_a)
     msg_b, out, merge = compute(
-        True, role_b, gates, kept, own, got_a, scale, sketches, got_b, half, carry, out
+        True,
+        role_b,
+        gates,
+        kept,
+        window(own, own_b, 4),
+        got_b,
+        scale,
+        window(sketches, first_b, 4),
+        carry,
+        out,
     )
     back_b = swapped(msg_b)
 

time: 109 us -> 109 us (level)
  the two profiles are of different devices: /device:TPU:0 before, /device:TPU:1 now
where the time goes in v1:
time: 109 us; the launch traced here: 107 us
  Pallas kernels  41.7 us (38%)
  waiting for transfers between devices  40.9 us (38%)
  starting transfers between devices  11.8 us (11%)
  local copies, waits for them, and re-layouts  10.9 us (10%)
  other arithmetic  1.81 us (2%)
    ppermute x5, waiting for transfers between devices, swapped(): return lax.ppermute(value, 'chain', [(i, i ^ 1) for i in range(chain)])  40.9 us
    pallas_call x2, Pallas kernels, compute(): pl.pallas_call(functools.partial(compute_kernel, second), out_shape=(part...  38.3 us
    ppermute x5, starting transfers between devices, swapped(): return lax.ppermute(value, 'chain', [(i, i ^ 1) for i in range(chain)])  9.83 us
    dynamic_slice x4, local copies, waits for them, and re-layouts, window(): return lax.dynamic_slice_in_dim(array, start, size, 0)  8.93 us
  transfers between devices with their start and end apart: 7, of which 3 were waited for; matrix products, arithmetic and copies ran while one was open for 10% of the time, Pallas kernels for 38%

profile of v1, /device:TPU:1, one launch (start us, length us, event | category | flops | bytes accessed | tf_op | source)
XLA Modules:
  0.0 107.4 jit_solution(478352500830572675)
XLA Ops:
  0.0 0.0 copy-start.6
  0.0 0.8 bitcast_select_fusion
  0.8 0.7 collective-permute-start.2
  1.5 1.3 %collective-permute-start.3 = (f32[16,256]{1,0:T(8,128)S(1)}, f32[16,256]{1,0:T(8,128)S(1)}, u32[]{:S(2)}, u32[]{:S(2)}) collective-permute-start(f32[16,256]{1,0:T(8,128)S(1)} %bitcast_select_fusion), channel_id=1, source_target_pairs={{4,8},{12,16},{20,24},{28,32},{36,40},{44,48},{52,56},{60,64},{68,... | collective-permute-start | bytes 49160 | tf_op jit(solution)/shard_map/ppermute | solution.py:458
  2.8 1.4 %pack.1 = bf16[5,1024,128]{2,1,0:T(8,128)(2,1)S(1)} custom-call(s32[1]{0:T(128)} %bitcast.1.role, bf16[16,1024,128]{2,1,0:T(8,128)(2,1)} %bitcast.36), custom_call_target="tpu_custom_call" | custom-call | tf_op jit(solution)/shard_map/pack/pallas_call | solution.py:335
  4.2 0.0 copy-start.7
  4.2 6.5 %collective-permute-start.4 = (bf16[5,1024,128]{2,1,0:T(8,128)(2,1)S(1)}, bf16[5,1024,128]{2,1,0:T(8,128)(2,1)}, u32[]{:S(2)}, u32[]{:S(2)}) collective-permute-start(bf16[5,1024,128]{2,1,0:T(8,128)(2,1)S(1)} %pack.1), channel_id=1, source_target_pairs={{0,4},{4,0},{8,12},{12,8},{16,20},{20,16},{24,28},{28,24},{32,36},... | collective-permute-start | bytes 3932168 | tf_op jit(solution)/shard_map/ppermute | solution.py:451
  10.7 0.0 copy-done.6
  10.7 0.1 collective-permute-start
  10.8 2.1 %constant_dynamic-slice_fusion.3 = bf16[3,1024,128]{2,1,0:T(8,128)(2,1)} fusion(bf16[16,1024,128]{2,1,0:T(8,128)(2,1)} %bitcast.37, s32[]{:T(128)} %mul.17), kind=kLoop, calls=%fused_computation.15 | loop fusion | bytes 1572868 | tf_op jit(solution)/shard_map/dynamic_slice | solution.py:465
  12.9 1.4 %collective-permute-start.1 = (bf16[3,1024,128]{2,1,0:T(8,128)(2,1)}, bf16[3,1024,128]{2,1,0:T(8,128)(2,1)}, u32[]{:S(2)}, u32[]{:S(2)}) collective-permute-start(bf16[3,1024,128]{2,1,0:T(8,128)(2,1)} %constant_dynamic-slice_fusion.3), channel_id=1, source_target_pairs={{0,4},{4,0},{8,12},{12,8},{16,20},{20,16},{24,28},{28,24},{32,36},... | collective-permute-start | bytes 2359304 | tf_op jit(solution)/shard_map/ppermute | solution.py:451
  14.4 0.0 copy-start.5
  14.4 0.0 copy-start.3
  14.4 0.0 copy-start.4
  14.4 1.6 %constant_dynamic-slice_fusion.1.refs_3_ = bf16[6,1024,128]{2,1,0:T(8,128)(2,1)S(1)} fusion(bf16[16,1024,128]{2,1,0:T(8,128)(2,1)} %bitcast.38, s32[]{:T(128)S(6)} %select_n.61), kind=kLoop, calls=%fused_computation.13 | loop fusion | bytes 3145732 | tf_op jit(solution)/shard_map/dynamic_slice | solution.py:465
  15.9 2.3 %constant_dynamic-slice_fusion.4.refs_3_ = bf16[4,1024,128]{2,1,0:T(8,128)(2,1)} fusion(bf16[16,1024,128]{2,1,0:T(8,128)(2,1)} %bitcast.39, s32[]{:T(128)S(6)} %select_n.53), kind=kLoop, calls=%fused_computation.16 | loop fusion | bytes 2097156 | tf_op jit(solution)/shard_map/dynamic_slice | solution.py:465
  18.2 0.1 pad_add_fusion.1.refs_0_
  18.3 0.1 pad_add_fusion.refs_0_
  18.3 0.0 copy-done.7
  18.4 0.6 slice.15
  19.0 3.0 %constant_dynamic-slice_fusion = (bf16[4,512,256]{2,1,0:T(8,128)(2,1)}, bf16[4,512,256]{2,1,0:T(8,128)(2,1)}) fusion(bf16[16,512,256]{2,1,0:T(8,128)(2,1)} %param.11, s32[]{:T(128)S(6)} %select_n.62, s32[]{:T(128)S(6)} %select_n.60), kind=kLoop, calls=%fused_computation.12 | loop fusion | bytes 4194312 | tf_op jit(solution)/shard_map/dynamic_slice | solution.py:465
  22.0 0.0 copy-done.5
  22.0 0.7 pad_maximum_fusion.refs_1_
  22.7 0.0 collective-permute-done.2
  22.8 0.0 collective-permute-done.3
  22.8 16.8 %collective-permute-done = f32[24,256]{1,0:T(8,128)S(1)} collective-permute-done((f32[24,256]{1,0:T(8,128)S(1)}, f32[24,256]{1,0:T(8,128)S(1)}, u32[]{:S(2)}, u32[]{:S(2)}) %collective-permute-start) | collective-permute-done | bytes 24608 | tf_op jit(solution)/shard_map/ppermute | solution.py:451
  39.5 0.0 copy-done.3
  39.5 0.0 copy-done.4
  39.5 0.1 select_bitcast_fusion.1
  39.6 0.1 broadcast_in_dim.8.refs_5_
  39.7 0.0 collective-permute-done.4.refs_4_
  39.7 0.0 copy-start.1
  39.7 1.2 %copy-done.1 = bf16[4,512,256]{2,1,0:T(8,128)(2,1)S(1)} copy-done((bf16[4,512,256]{2,1,0:T(8,128)(2,1)S(1)}, bf16[4,512,256]{2,1,0:T(8,128)(2,1)}, u32[]{:S(2)}) %copy-start.1) | copy-done | bytes 1048600
  40.9 0.0 copy-start
  41.0 0.0 copy-start.2
  41.0 19.5 %first_half.1 = (bf16[4,1024,128]{2,1,0:T(8,128)(2,1)}, bf16[16,1024,128]{2,1,0:T(8,128)(2,1)}, bf16[7,256,256]{2,1,0:T(8,128)(2,1)S(1)}) custom-call(s32[3]{0:T(128)S(1)} %pad_add_fusion.1.refs_0_, f32[5]{0:T(128)S(1)} %pad_maximum_fusion.refs_1_, s32[16]{0:T(128)S(1)} %fusion.1.refs_2_, bf16[6,1024,128]{2,1,0:T(8,128)(2,1)S(1)} %constant_dynamic-slice_fusion.1.refs_3_, ...), custom_call_target="tpu_custom_call" | custom-call | flops 20000000000 | bytes 8000000 | tf_op jit(solution)/shard_map/first_half/pallas_call | solution.py:367
  60.5 1.4 %collective-permute-start.6 = (bf16[4,1024,128]{2,1,0:T(8,128)(2,1)}, bf16[4,1024,128]{2,1,0:T(8,128)(2,1)S(1)}, u32[]{:S(2)}, u32[]{:S(2)}) collective-permute-start(bf16[4,1024,128]{2,1,0:T(8,128)(2,1)} %get-tuple-element.14), channel_id=1, source_target_pairs={{0,4},{4,0},{8,12},{12,8},{16,20},{20,16},{24,28},{28,24},{32,36},... | collective-permute-start | bytes 3145736 | tf_op jit(solution)/shard_map/ppermute | solution.py:451
  62.0 0.0 collective-permute-done.1.refs_4_
  62.0 0.0 copy-done
  62.0 0.0 copy-done.2
  62.0 18.8 %second_half.1 = (bf16[4,1024,128]{2,1,0:T(8,128)(2,1)}, bf16[16,1024,128]{2,1,0:T(8,128)(2,1)}, bf16[1024,128]{1,0:T(8,128)(2,1)S(1)}) custom-call(s32[3]{0:T(128)S(1)} %pad_add_fusion.refs_0_, f32[5]{0:T(128)S(1)} %pad_maximum_fusion.refs_1_, s32[16]{0:T(128)S(1)} %fusion.1.refs_2_, ...), custom_call_target="tpu_custom_call", output_to_operand_aliasing={{1}: (8, {})} | custom-call | flops 20000000000 | bytes 8000000 | tf_op jit(solution)/shard_map/second_half/pallas_call | solution.py:367
  80.8 0.4 collective-permute-start.5
  81.1 2.0 %collective-permute-done.6.block = bf16[4,1024,128]{2,1,0:T(8,128)(2,1)S(1)} collective-permute-done((bf16[4,1024,128]{2,1,0:T(8,128)(2,1)}, bf16[4,1024,128]{2,1,0:T(8,128)(2,1)S(1)}, u32[]{:S(2)}, u32[]{:S(2)}) %collective-permute-start.6) | collective-permute-done | bytes 1048608 | tf_op jit(solution)/shard_map/ppermute | solution.py:451
  83.1 1.0 place.2.refs_0_
  84.1 22.1 %collective-permute-done.5.block = bf16[4,1024,128]{2,1,0:T(8,128)(2,1)S(1)} collective-permute-done((bf16[4,1024,128]{2,1,0:T(8,128)(2,1)}, bf16[4,1024,128]{2,1,0:T(8,128)(2,1)S(1)}, u32[]{:S(2)}, u32[]{:S(2)}) %collective-permute-start.5) | collective-permute-done | bytes 1048608 | tf_op jit(solution)/shard_map/ppermute | solution.py:451
  106.2 1.0 place.3
  (6 shorter events, 0.0 us)
Async XLA Ops:
  0.0 10.7 %copy-start.6 = (s32[1,1,16]{2,1,0:T(1,128)S(1)}, s32[1,1,16]{2,1,0:T(1,128)}, u32[]{:S(2)}) copy-start(s32[1,1,16]{2,1,0:T(1,128)} %param.10) | copy-start | bytes 196
  0.8 21.9 %collective-permute-start.2 = (f32[16,256]{1,0:T(8,128)S(1)}, f32[16,256]{1,0:T(8,128)S(1)}, u32[]{:S(2)}, u32[]{:S(2)}) collective-permute-start(f32[16,256]{1,0:T(8,128)S(1)} %bitcast_select_fusion), channel_id=1, source_target_pairs={{4,12},{12,20},{20,28},{28,36},{36,44},{44,52},{52,60},{60,68},{68... | collective-permute-start | bytes 49160 | tf_op jit(solution)/shard_map/ppermute | solution.py:458
  1.5 21.3 %collective-permute-start.3 = (f32[16,256]{1,0:T(8,128)S(1)}, f32[16,256]{1,0:T(8,128)S(1)}, u32[]{:S(2)}, u32[]{:S(2)}) collective-permute-start(f32[16,256]{1,0:T(8,128)S(1)} %bitcast_select_fusion), channel_id=1, source_target_pairs={{4,8},{12,16},{20,24},{28,32},{36,40},{44,48},{52,56},{60,64},{68,... | collective-permute-start | bytes 49160 | tf_op jit(solution)/shard_map/ppermute | solution.py:458
  4.2 14.1 %copy-start.7 = (f32[3]{0:T(128)S(1)}, f32[3]{0:T(128)}, u32[]{:S(2)}) copy-start(f32[3]{0:T(128)} %param.13) | copy-start | bytes 40
  4.2 35.5 %collective-permute-start.4 = (bf16[5,1024,128]{2,1,0:T(8,128)(2,1)S(1)}, bf16[5,1024,128]{2,1,0:T(8,128)(2,1)}, u32[]{:S(2)}, u32[]{:S(2)}) collective-permute-start(bf16[5,1024,128]{2,1,0:T(8,128)(2,1)S(1)} %pack.1), channel_id=1, source_target_pairs={{0,4},{4,0},{8,12},{12,8},{16,20},{20,16},{24,28},{28,24},{32,36},... | collective-permute-start | bytes 3932168 | tf_op jit(solution)/shard_map/ppermute | solution.py:451
  10.7 28.8 %collective-permute-start = (f32[24,256]{1,0:T(8,128)S(1)}, f32[24,256]{1,0:T(8,128)S(1)}, u32[]{:S(2)}, u32[]{:S(2)}) collective-permute-start(f32[24,256]{1,0:T(8,128)S(1)} %select_maximum_fusion.2), channel_id=1, source_target_pairs={{0,4},{4,0},{8,12},{12,8},{16,20},{20,16},{24,28},{28,24},{32,36},... | collective-permute-start | bytes 73736 | tf_op jit(solution)/shard_map/ppermute | solution.py:451
  12.9 49.0 %collective-permute-start.1 = (bf16[3,1024,128]{2,1,0:T(8,128)(2,1)}, bf16[3,1024,128]{2,1,0:T(8,128)(2,1)}, u32[]{:S(2)}, u32[]{:S(2)}) collective-permute-start(bf16[3,1024,128]{2,1,0:T(8,128)(2,1)} %constant_dynamic-slice_fusion.3), channel_id=1, source_target_pairs={{0,4},{4,0},{8,12},{12,8},{16,20},{20,16},{24,28},{28,24},{32,36},... | collective-permute-start | bytes 2359304 | tf_op jit(solution)/shard_map/ppermute | solution.py:451
  14.4 7.6 %copy-start.5 = (f32[2]{0:T(128)S(1)}, f32[2]{0:T(128)}, u32[]{:S(2)}) copy-start(f32[2]{0:T(128)} %param.12) | copy-start | bytes 28
  14.4 25.2 %copy-start.3 = (f32[1,1,16,256]{3,2,1,0:T(8,128)S(1)}, f32[1,1,16,256]{3,2,1,0:T(8,128)}, u32[]{:S(2)}) copy-start(f32[1,1,16,256]{3,2,1,0:T(8,128)} %param.8) | copy-start | bytes 49156
  14.4 25.2 %copy-start.4 = (s32[1,1,16]{2,1,0:T(1,128)S(1)}, s32[1,1,16]{2,1,0:T(1,128)}, u32[]{:S(2)}) copy-start(s32[1,1,16]{2,1,0:T(1,128)} %param.9) | copy-start | bytes 196
  39.7 1.2 %copy-start.1 = (bf16[4,512,256]{2,1,0:T(8,128)(2,1)S(1)}, bf16[4,512,256]{2,1,0:T(8,128)(2,1)}, u32[]{:S(2)}) copy-start(bf16[4,512,256]{2,1,0:T(8,128)(2,1)} %get-tuple-element.17.refs_6_) | copy-start | bytes 3145732
  40.9 21.0 %copy-start = (bf16[4,512,256]{2,1,0:T(8,128)(2,1)S(1)}, bf16[4,512,256]{2,1,0:T(8,128)(2,1)}, u32[]{:S(2)}) copy-start(bf16[4,512,256]{2,1,0:T(8,128)(2,1)} %get-tuple-element.18.refs_6_) | copy-start | bytes 3145732
  41.0 21.0 %copy-start.2 = (bf16[4,1024,128]{2,1,0:T(8,128)(2,1)S(1)}, bf16[4,1024,128]{2,1,0:T(8,128)(2,1)}, u32[]{:S(2)}) copy-start(bf16[4,1024,128]{2,1,0:T(8,128)(2,1)} %constant_dynamic-slice_fusion.4.refs_3_) | copy-start | bytes 3145732
  60.5 22.6 %collective-permute-start.6 = (bf16[4,1024,128]{2,1,0:T(8,128)(2,1)}, bf16[4,1024,128]{2,1,0:T(8,128)(2,1)S(1)}, u32[]{:S(2)}, u32[]{:S(2)}) collective-permute-start(bf16[4,1024,128]{2,1,0:T(8,128)(2,1)} %get-tuple-element.14), channel_id=1, source_target_pairs={{0,4},{4,0},{8,12},{12,8},{16,20},{20,16},{24,28},{28,24},{32,36},... | collective-permute-start | bytes 3145736 | tf_op jit(solution)/shard_map/ppermute | solution.py:451
  80.8 25.5 %collective-permute-start.5 = (bf16[4,1024,128]{2,1,0:T(8,128)(2,1)}, bf16[4,1024,128]{2,1,0:T(8,128)(2,1)S(1)}, u32[]{:S(2)}, u32[]{:S(2)}) collective-permute-start(bf16[4,1024,128]{2,1,0:T(8,128)(2,1)} %get-tuple-element.13), channel_id=1, source_target_pairs={{0,4},{4,0},{8,12},{12,8},{16,20},{20,16},{24,28},{28,24},{32,36},... | collective-permute-start | bytes 3145736 | tf_op jit(solution)/shard_map/ppermute | solution.py:451

commit v2 on v1

v2 whole, which is shorter than its diff:
```python
import functools

import jax
import jax.numpy as jnp
from jax import lax
from jax.experimental import pallas as pl
from jax.experimental.pallas import tpu as pltpu
from jax.sharding import PartitionSpec as P

f32 = jnp.float32
bf16 = jnp.bfloat16


BATCH = 4
LEAF = 32
PANELS = 8
LANES = 128
SIZE = 256


def split(x):
    high = x.astype(bf16)
    return high, (x - high.astype(f32)).astype(bf16)


def invert_leaf(d):
    lane = lax.broadcasted_iota(jnp.int32, (8, LANES), 1)
    sub = lax.broadcasted_iota(jnp.int32, (8, LANES), 0)
    segment = (lane // LEAF) * LEAF
    tiles = LEAF // 8
    rows = [d[8 * t : 8 * t + 8, :] for t in range(tiles)]
    cols = [
        [
            jnp.take_along_axis(rows[t], segment + j, axis=1) if t >= j // 8 else None
            for t in range(tiles)
        ]
        for j in range(LEAF)
    ]
    inverse = [((lane - segment) == (sub + 8 * t)).astype(f32) for t in range(tiles)]
    pivots = [jnp.ones((8, LANES), f32) for _ in range(tiles)]

    def row(v, r):
        return jnp.broadcast_to(v[r : r + 1, :], (8, LANES))

    for j in range(LEAF):
        top, r = j // 8, j % 8
        pivot = row(cols[j][top], r)
        reciprocal = 1.0 / pivot
        pivots[top] = jnp.where(sub == r, pivot, pivots[top])
        scaled = {t: cols[j][t] * reciprocal for t in range(top, tiles)}
        for i in range(j + 1, LEAF):
            factor = row(scaled[i // 8], i % 8)
            for t in range(i // 8, tiles):
                cols[i][t] = cols[i][t] - factor * cols[j][t]
        source = row(inverse[top], r)
        for t in range(top, tiles):
            factor = jnp.where(sub > r, scaled[t], 0.0) if t == top else scaled[t]
            inverse[t] = inverse[t] - factor * source
    return jnp.concatenate([inverse[t] * lax.rsqrt(pivots[t]) for t in range(tiles)], axis=0)


def block_weights(high, low, masks):
    high = jnp.concatenate([high * mask for mask in masks], axis=0)
    low = jnp.concatenate([low * mask for mask in masks], axis=0)
    upper = jnp.concatenate([high, high], axis=1)
    lower = jnp.concatenate([low, jnp.zeros_like(low)], axis=1)
    return jnp.concatenate([upper, lower], axis=0)


def times_transposed(x, weights):
    out = lax.dot_general(x, weights, (((1,), (1,)), ((), ())), preferred_element_type=f32)
    return out[:, :LANES] + out[:, LANES:]


def invert_factor(a_ref, x_ref):
    lane = lax.broadcasted_iota(jnp.int32, (LEAF, LANES), 1)
    sub = lax.broadcasted_iota(jnp.int32, (LEAF, LANES), 0)
    eye = ((lane % LEAF) == sub).astype(f32)
    masks = [((lane // LEAF) == b).astype(f32).astype(bf16) for b in range(BATCH)]

    def weights_of(rows, ks):
        return jnp.concatenate(
            [
                block_weights(
                    x_ref[rows, k * SIZE : k * SIZE + LANES],
                    x_ref[rows, k * SIZE + LANES : (k + 1) * SIZE],
                    masks,
                )
                for k in ks
            ],
            axis=1,
        )

    partial = None
    for j in range(PANELS):
        start = j * LEAF
        block = slice(start, start + LEAF)
        col = a_ref[j]
        if j:
            last = slice((j - 1) * SIZE, j * SIZE)
            if partial is not None:
                col = col - partial
            col = col - times_transposed(x_ref[:, last], weights_of(block, [j - 1]))
            x_ref[block, : j * SIZE] = jnp.zeros((LEAF, j * SIZE), bf16)
            if j < PANELS - 1:
                following = slice(start + LEAF, start + 2 * LEAF)
                partial = times_transposed(
                    x_ref[:, : j * SIZE], weights_of(following, range(j))
                )
        inverse = invert_leaf(col[block])
        col = jnp.concatenate(
            [part for part in (col[:start], eye, col[start + LEAF :]) if part.shape[0]], axis=0
        )
        col = times_transposed(
            jnp.concatenate(split(col), axis=1), block_weights(*split(inverse), masks)
        )
        x_ref[:, j * SIZE : (j + 1) * SIZE] = jnp.concatenate(split(col), axis=1)


UPPER, LOWER = slice(0, SIZE), slice(SIZE, 2 * SIZE)
CONTRACT_ROWS = (((0,), (0,)), ((), ()))


def dot(a, b):
    return jnp.dot(a, b, preferred_element_type=f32)


def lines_of(lane_block, s):
    return pl.ds(2 * lane_block + s, SIZE, stride=4)


def lanes_of(lane_block):
    return slice(lane_block * LANES, (lane_block + 1) * LANES)


def column_of(line):
    return jnp.transpose(jnp.broadcast_to(line, (LANES, SIZE)))


def weigh(t, role, own, got, scale, left, right, wide):
    is_right = role[0] == 1
    q = role[1] - 1 + t
    own_wide = own[jnp.clip(q, 0, 15) - role[2]].astype(f32)
    got_wide = got[...].astype(f32)
    wide[0] = jnp.where(is_right, got_wide, own_wide)
    wide[1] = jnp.where(is_right, own_wide, got_wide)
    left_rows = column_of(scale[0, q + 1])
    right_rows = column_of(scale[1, q + 1])
    for s in range(2):
        col = scale[2, q + s + 1]
        for jb in range(2):
            lines, lanes = lines_of(jb, s), lanes_of(jb)
            left[s, :, lanes] = (wide[0, lines, :] * left_rows).astype(bf16)
            right[s, :, lanes] = ((wide[1, lines, :] * right_rows) * col[:, lanes]).astype(bf16)


def sample(gates, kept, sketch, left, before, right, right_before, right_after, mixed, samp, gram):
    g0, g1, p0, p1, p2 = [gates[i] for i in range(5)]
    mixed[UPPER, UPPER] = (g0 * dot(left[0], right[0])).astype(bf16)
    mixed[UPPER, LOWER] = (p0 * dot(left[0], right[1]) + p2 * dot(left[1], right_after)).astype(bf16)
    mixed[LOWER, UPPER] = (
        p2 * dot(before[0], right_before) + p1 * dot(before[1], right[0])
    ).astype(bf16)
    mixed[LOWER, LOWER] = (g1 * dot(before[1], right[1])).astype(bf16)
    keep = lax.broadcasted_iota(jnp.int32, (1, SIZE), 1) < kept
    sampled = jnp.where(keep, dot(mixed[...], sketch), 0.0)
    high, low = split(sampled)
    samp[0] = high
    samp[1] = low
    shift = 0.01 * jnp.sum(sampled * sampled) / SIZE
    hh = lax.dot_general(high, high, CONTRACT_ROWS, preferred_element_type=f32)
    hl = lax.dot_general(high, low, CONTRACT_ROWS, preferred_element_type=f32)
    rows = lax.broadcasted_iota(jnp.int32, (SIZE, SIZE), 0)
    eye = rows == lax.broadcasted_iota(jnp.int32, (SIZE, SIZE), 1)
    added = jnp.where(keep, 0.0, 1.0) + shift
    gram[...] = (hh + (hl + jnp.transpose(hl))) + jnp.where(eye, added, 0.0)


def rolled(value, segments):
    shift = (segments * LEAF) % LANES
    return pltpu.roll(value, shift, axis=1) if shift else value


def gather_lanes(pieces):
    segment = lax.broadcasted_iota(jnp.int32, (1, LANES), 1) // LEAF
    out = pieces[0]
    for i in range(1, BATCH):
        out = jnp.where(segment == i, pieces[i], out)
    return out


def solve(gram, samp, scaled, a_ref, x_ref):
    for k in range(PANELS):
        rows = slice(k * LEAF, SIZE)
        lanes = lanes_of(k // 4)
        a_ref[k, rows, :] = gather_lanes(
            [rolled(gram[b][rows, lanes], b - k % 4) for b in range(BATCH)]
        )
        if k:
            a_ref[k, : k * LEAF, :] = jnp.zeros((k * LEAF, LANES), f32)

    invert_factor(a_ref, x_ref)

    def factor(b, offset):
        halves = []
        for g in range(2):
            panels = [
                rolled(x_ref[:, k * SIZE + offset : k * SIZE + offset + LANES], k % 4 - b)
                for k in range(4 * g, 4 * g + 4)
            ]
            halves.append(gather_lanes(panels))
        return jnp.concatenate(halves, axis=1)

    for b in range(BATCH):
        high, low = factor(b, 0), factor(b, LANES)
        solved = dot(samp[b][0], high) + (dot(samp[b][0], low) + dot(samp[b][1], high))
        scaled[b] = (solved * 16.0).astype(bf16)


def deliver(role, scaled, mixed, wide, ready, msg, out, sems):
    is_right = role[0] == 1
    copies = []
    for b in range(BATCH):
        right_part = lax.dot_general(
            scaled[b], mixed[b][...], CONTRACT_ROWS, preferred_element_type=f32
        ) * (1.0 / SIZE)
        left_wide, right_wide = wide.at[2 * (b % 2)], wide.at[2 * (b % 2) + 1]
        for s in range(2):
            half = scaled[b, UPPER, :] if s == 0 else scaled[b + 1, LOWER, :]
            for jb in range(2):
                lines = lines_of(jb, s)
                left_wide[lines, :] = half[:, lanes_of(jb)].astype(f32)
                right_wide[lines, :] = right_part[:, lanes_of(2 * s + jb)]
        left_site = left_wide[...]
        right_site = right_wide[...]
        ready[0, b] = jnp.where(is_right, left_site, right_site).astype(bf16)
        ready[1, b] = jnp.where(is_right, right_site, left_site).astype(bf16)
        for which, target in enumerate((msg.at[b], out.at[role[1] + b])):
            copies.append(
                pltpu.make_async_copy(ready.at[which, b], target, sems.at[which, b])
            )
            copies[-1].start()
    return copies


def early_kernel(role, gates, kept, own, got, scale, sketch, *refs):
    mixed, samp, gram, edge, left_w, right_w, wide = refs

    def step(t, loop):
        at = jnp.minimum(t - 1, 3)
        weigh(t, role, own, got.at[at], scale, left_w.at[t], right_w.at[t], wide)
        return loop

    lax.fori_loop(1, 6, step, 0)
    for s in range(2):
        edge[s] = left_w[1, s]
        edge[2 + s] = right_w[1, s]
    edge[4] = right_w[2, 0]
    below = role[1] - 5
    wide[0] = got[3].astype(f32)
    rows = column_of(scale[1, below + 1])
    col = scale[2, below + 2]
    for jb in range(2):
        lanes = lanes_of(jb)
        edge[5, :, lanes] = ((wide[0, lines_of(jb, 1), :] * rows) * col[:, lanes]).astype(bf16)
    for b in range(1, BATCH):
        t = b + 1
        sample(
            gates,
            kept[role[1] + b],
            sketch[b],
            (left_w[t, 0], left_w[t, 1]),
            (left_w[t - 1, 0], left_w[t - 1, 1]),
            (right_w[t, 0], right_w[t, 1]),
            right_w[t - 1, 1],
            right_w[t + 1, 0],
            mixed.at[b - 1],
            samp.at[b - 1],
            gram.at[b - 1],
        )


def first_kernel(role, gates, kept, own, got, scale, sketch, *refs):
    (mixed_e, samp_e, gram_e, edge, msg, out, carry), refs = refs[:7], refs[7:]
    mixed, samp, gram, scaled, a_ref, x_ref, wide, ready, sems = refs
    left, right = carry.at[pl.ds(1, 2)], carry.at[pl.ds(3, 2)]
    weigh(0, role, own, got.at[0], scale, left, right, wide)
    sample(
        gates,
        kept[role[1]],
        sketch[0],
        (edge[0], edge[1]),
        (left[0], left[1]),
        (edge[2], edge[3]),
        right[1],
        edge[4],
        mixed,
        samp,
        gram,
    )
    mixed = [mixed] + [mixed_e.at[b] for b in range(BATCH - 1)]
    samp = [samp] + [samp_e.at[b] for b in range(BATCH - 1)]
    gram = [gram] + [gram_e.at[b] for b in range(BATCH - 1)]
    solve(gram, samp, scaled, a_ref, x_ref)
    scaled[BATCH, LOWER, :] = jnp.zeros((SIZE, SIZE), bf16)
    carry[0] = scaled[0, LOWER, :]
    for copy in deliver(role, scaled, mixed, wide, ready, msg, out, sems):
        copy.wait()


def second_kernel(role, gates, kept, own, got, scale, sketch, *refs):
    (edge, carry, _, msg, out, merge), refs = refs[:6], refs[6:]
    left_w, right_w, mixed, samp, gram, scaled, a_ref, x_ref, wide = refs[:9]
    ready, sems = refs[9:]

    def step(t, loop):
        at = jnp.maximum(t - 1, 0)
        weigh(t, role, own, got.at[at], scale, left_w.at[t], right_w.at[t], wide)
        return loop

    lax.fori_loop(0, 4, step, 0)
    right_w[0, 1] = edge[5]
    for s in range(2):
        left_w[4, s] = carry[1 + s]
        right_w[4, s] = carry[3 + s]
    right_w[5, 0] = edge[2]
    for b in range(BATCH):
        t = b + 1
        sample(
            gates,
            kept[role[1] + b],
            sketch[b],
            (left_w[t, 0], left_w[t, 1]),
            (left_w[b, 0], left_w[b, 1]),
            (right_w[t, 0], right_w[t, 1]),
            right_w[b, 1],
            right_w[t + 1, 0],
            mixed.at[b],
            samp.at[b],
            gram.at[b],
        )
    every = range(BATCH)
    solve([gram.at[b] for b in every], [samp.at[b] for b in every], scaled, a_ref, x_ref)
    scaled[BATCH, LOWER, :] = carry[0]
    copies = deliver(
        role, scaled, [mixed.at[b] for b in every], wide, ready, msg, out, sems
    )
    used = jnp.where(role[0] == 1, 0.0, 1.0)
    for jb in range(2):
        value = scaled[0, LOWER, lanes_of(jb)].astype(f32)
        wide[0, lines_of(jb, 0), :] = jnp.zeros((SIZE, LANES), f32)
        wide[0, lines_of(jb, 1), :] = value * used
    merge[...] = wide[0].astype(bf16)
    for copy in copies:
        copy.wait()


def in_hbm(x):
    return pltpu.with_memory_space_constraint(x, pltpu.HBM)


def shaped(*shape, dtype=bf16):
    return jax.ShapeDtypeStruct(shape, dtype)


def run(kernel, operands, specs, outs, out_specs, scratch, aliases=None, mib=20):
    return pl.pallas_call(
        kernel,
        out_shape=outs,
        in_specs=specs,
        out_specs=out_specs,
        scratch_shapes=scratch,
        input_output_aliases=aliases or {},
        compiler_params=pltpu.CompilerParams(vmem_limit_bytes=mib * 2**20),
        cost_estimate=pl.CostEstimate(
            flops=mib * 500_000_000, bytes_accessed=8_000_000, transcendentals=0
        ),
    )(*operands)


SMEM = pl.BlockSpec(memory_space=pltpu.SMEM)
VMEM = pl.BlockSpec(memory_space=pltpu.VMEM)
HBM = pl.BlockSpec(memory_space=pltpu.HBM)
SECTOR = (4 * SIZE, LANES)


def factor_scratch():
    return [
        pltpu.VMEM((BATCH + 1, 2 * SIZE, SIZE), bf16),
        pltpu.VMEM((PANELS, SIZE, LANES), f32),
        pltpu.VMEM((SIZE, PANELS * SIZE), bf16),
        pltpu.VMEM((4, *SECTOR), f32),
    ]


def sample_shapes(make, *lead):
    return [
        make((*lead, 2 * SIZE, 2 * SIZE), bf16),
        make((*lead, 2, 2 * SIZE, SIZE), bf16),
        make((*lead, SIZE, SIZE), f32),
    ]


def early(role, gates, kept, own, got, scale, sketch):
    return run(
        early_kernel,
        (role, gates, kept, own, got, scale, sketch),
        [SMEM] * 3 + [VMEM] * 4,
        sample_shapes(jax.ShapeDtypeStruct, BATCH - 1) + [shaped(6, SIZE, SIZE)],
        [VMEM] * 4,
        [
            pltpu.VMEM((6, 2, SIZE, SIZE), bf16),
            pltpu.VMEM((6, 2, SIZE, SIZE), bf16),
            pltpu.VMEM((2, *SECTOR), f32),
        ],
    )


def first_half(role, gates, kept, own, got, scale, sketch, parts):
    return run(
        first_kernel,
        (role, gates, kept, own, got, scale, sketch, *parts),
        [SMEM] * 3 + [VMEM] * 8,
        [shaped(BATCH, *SECTOR), shaped(16, *SECTOR), shaped(5, SIZE, SIZE)],
        [HBM, HBM, VMEM],
        sample_shapes(pltpu.VMEM)
        + factor_scratch()
        + [pltpu.VMEM((2, BATCH, *SECTOR), bf16), pltpu.SemaphoreType.DMA((2, BATCH))],
    )


def second_half(role, gates, kept, own, got, scale, sketch, edge, carry, out):
    return run(
        second_kernel,
        (role, gates, kept, own, got, scale, sketch, edge, carry, out),
        [SMEM] * 3 + [VMEM] * 6 + [HBM],
        [shaped(BATCH, *SECTOR), shaped(16, *SECTOR), shaped(*SECTOR)],
        [HBM, HBM, VMEM],
        [pltpu.VMEM((6, 2, SIZE, SIZE), bf16), pltpu.VMEM((6, 2, SIZE, SIZE), bf16)]
        + sample_shapes(pltpu.VMEM, BATCH)
        + factor_scratch()
        + [
            pltpu.VMEM((2, BATCH, *SECTOR), bf16),
            pltpu.SemaphoreType.DMA((2, BATCH)),
        ],
        aliases={9: 1},
    )


def pack_kernel(role, sizes, kept, lam, own, out, low, packed, both, sems):
    flag = role[0]
    copies = [
        pltpu.make_async_copy(own.at[7 + 8 * flag], both.at[0], sems.at[0]),
        pltpu.make_async_copy(own.at[7], both.at[1], sems.at[1]),
        pltpu.make_async_copy(own.at[pl.ds(4 + 8 * flag, 3)], out.at[pl.ds(0, 3)], sems.at[2]),
        pltpu.make_async_copy(own.at[3 + 8 * flag], low.at[0], sems.at[3]),
    ]
    for copy in copies:
        copy.start()
    lane = lax.broadcasted_iota(jnp.int32, (1, SIZE), 1)
    line = jnp.zeros((1, SIZE), f32)
    for q in range(16):
        packed[q : q + 1, :] = jnp.where(lane < sizes[q], lam[q : q + 1, :], 0.0)
        line = jnp.where(lane == q, kept[q].astype(f32), line)
    packed[16:24, :] = jnp.broadcast_to(line, (8, SIZE))
    copies[0].wait()
    copies[1].wait()
    is_odd = lax.broadcasted_iota(jnp.int32, SECTOR, 0) % 2 == 1
    out[3] = jnp.where(is_odd, both[1].astype(f32), both[0].astype(f32)).astype(bf16)
    copies[2].wait()
    copies[3].wait()


def pack(role, sizes, kept, lam, own):
    return run(
        pack_kernel,
        (role, sizes, kept, lam, in_hbm(own)),
        [SMEM] * 3 + [VMEM, HBM],
        [shaped(4, *SECTOR), shaped(1, *SECTOR), shaped(24, SIZE, dtype=f32)],
        [VMEM] * 3,
        [pltpu.VMEM((2, *SECTOR), bf16), pltpu.SemaphoreType.DMA((4,))],
        mib=2,
    )


def place_kernel(merged, at, block, *refs):
    if merged:
        merge, _, out, last, sems = refs
    else:
        _, out, sems = refs
    count = block.shape[0]
    copies = []
    for b in range(count):
        source = block.at[b]
        if merged and b == count - 1:
            last[...] = block[b] + merge[...]
            source = last
        copies.append(pltpu.make_async_copy(source, out.at[at[0] + b], sems.at[b]))
        copies[-1].start()
    for copy in copies:
        copy.wait()


def place(out, block, at, merge=None):
    smem = pl.BlockSpec(memory_space=pltpu.SMEM)
    vmem = pl.BlockSpec(memory_space=pltpu.VMEM)
    hbm = pl.BlockSpec(memory_space=pltpu.HBM)
    operands = (jnp.reshape(at, (1,)), block) + (() if merge is None else (merge,)) + (out,)
    scratch = [] if merge is None else [pltpu.VMEM(merge.shape, bf16)]
    return pl.pallas_call(
        functools.partial(place_kernel, merge is not None),
        out_shape=jax.ShapeDtypeStruct(out.shape, out.dtype),
        in_specs=[smem] + [vmem] * (len(operands) - 2) + [hbm],
        out_specs=hbm,
        scratch_shapes=scratch + [pltpu.SemaphoreType.DMA((block.shape[0],))],
        input_output_aliases={len(operands) - 1: 0},
        compiler_params=pltpu.CompilerParams(vmem_limit_bytes=8 * 2**20),
        cost_estimate=pl.CostEstimate(flops=1000000, bytes_accessed=2_000_000, transcendentals=0),
        name="place",
    )(*operands)


def to_lines(x):
    n = x.shape[0]
    return x.reshape(n, SIZE, 2, 2, LANES).transpose(0, 1, 3, 2, 4).reshape(n, 4 * SIZE, LANES)


def from_lines(x):
    n = x.shape[0]
    return x.reshape(n, SIZE, 2, 2, LANES).transpose(0, 1, 3, 2, 4).reshape(n, SIZE, 2, SIZE)


def shards(site_tensors, bond_weights, sector_sizes, kept_ranks, sketches, gate_ends, gate_pair):
    chain = lax.axis_size("chain")
    count = lax.axis_size("group") * chain
    site = lax.axis_index("group") * chain + lax.axis_index("chain")
    is_right = site % 2 == 1

    def swapped(value):
        return lax.ppermute(value, "chain", [(i, i ^ 1) for i in range(chain)])

    def onward(value, by):
        def place(n):
            return n % chain * (count // chain) + n // chain

        pairs = [(place(i), place(i + by)) for i in range(1, count, 2) if i + by < count]
        return lax.ppermute(value, ("chain", "group"), pairs)

    own = to_lines(site_tensors[0, 0])
    sectors = own.shape[0]
    flag = is_right.astype(jnp.int32)

    def window(array, start, size):
        return lax.dynamic_slice_in_dim(array, start, size, 0)

    outgoing, outgoing_low, packed = pack(
        jnp.reshape(flag, (1,)), sector_sizes[0, 0], kept_ranks[0, 0], bond_weights[0, 0], own
    )
    lam = packed[:sectors]
    other = swapped(packed)
    got_a = swapped(outgoing)
    got_low = swapped(outgoing_low)
    before_left = onward(lam, 1)
    before_right = onward(lam, 2)
    got_b = swapped(window(own, 8 * flag, 3))

    lam_prev = jnp.where(is_right, before_right, before_left)
    lam_prev = jnp.where(site < 2, jnp.ones_like(lam), lam_prev)
    lam_mid = jnp.where(is_right, other[:sectors], lam)
    lam_next = jnp.where(is_right, lam, other[:sectors])
    scale = jnp.pad(jnp.stack([lam_prev, lam_mid, lam_next]), ((0, 0), (1, 7), (0, 0)))
    scale = scale[:, :, None, :]
    kept = jnp.where(is_right, other[sectors, :sectors], packed[sectors, :sectors]).astype(jnp.int32)
    gates = jnp.concatenate([gate_ends, 1.0 + gate_pair[:2], gate_pair[2:]])
    first_a = 12 - 8 * flag
    first_b = 8 - 8 * flag
    own_a = 10 - 7 * flag
    own_b = 7 - 7 * flag
    role_a = jnp.stack([flag, first_a, own_a])
    role_b = jnp.stack([flag, first_b, own_b])

    own_win = window(own, own_a, 6)
    sketch_win = window(sketches, first_a, BATCH)
    parts = early(role_a, gates, kept, own_win, got_a, scale, sketch_win)
    msg_a, out, carry = first_half(
        role_a, gates, kept, own_win, got_low, scale, sketch_win, parts
    )
    back_a = swapped(msg_a)
    own_win = window(own, own_b, BATCH)
    sketch_win = window(sketches, first_b, BATCH)
    msg_b, out, merge = second_half(
        role_b, gates, kept, own_win, got_b, scale, sketch_win, parts[3], carry, out
    )
    back_b = swapped(msg_b)

    back_at = 8 * flag
    out = place(out, back_a, back_at + 4, merge)
    out = place(out, back_b, back_at)
    return from_lines(out)[None, None]


def solution(mesh):
    return jax.shard_map(
        shards,
        mesh=mesh,
        in_specs=(
            P("group", "chain", None, None, None, None),
            P("group", "chain", None, None),
            P("group", "chain", None),
            P("group", "chain", None),
            P(),
            P(),
            P(),
        ),
        out_specs=P("group", "chain", None, None, None, None),
        check_vma=False,
    )
```

time: 109 us -> 121 us (1.11)
  starting transfers between devices: 11.8 us -> 26.2 us
  waiting for transfers between devices: 40.9 us -> 38.5 us
  local copies, waits for them, and re-layouts: 10.9 us -> 12.4 us
    ppermute x5 -> x6, waiting for transfers between devices: 40.9 us -> 25.8 us  [swapped(): return lax.ppermute(value, 'chain', [(i, i ^ 1) for i in range(chain)])]
    ppermute x5 -> x6, starting transfers between devices: 9.83 us -> 24.3 us  [swapped(): return lax.ppermute(value, 'chain', [(i, i ^ 1) for i in range(chain)])]
    ppermute x2, waiting for transfers between devices: 0.01 us -> 12.7 us  [onward(): return lax.ppermute(value, ('chain', 'group'), pairs)]
    unnamed x16, local copies, waits for them, and re-layouts: 1.25 us -> 3.27 us
    pallas_call x3 -> x4, Pallas kernels: 39.8 us -> 39.2 us  [run(): pl.pallas_call(kernel, out_shape=outs, in_specs=specs, out_specs=out_spec...]
  transfers between devices with their start and end apart: 7 -> 8, of which waited for: 3 -> 3; matrix products, arithmetic and copies ran while one was open for 10% -> 8% of each run, Pallas kernels for 38% -> 31%
where the time goes in v2:
time: 121 us; the launch traced here: 120 us
  Pallas kernels  41.1 us (34%)
  waiting for transfers between devices  38.5 us (32%)
  starting transfers between devices  26.2 us (22%)
  local copies, waits for them, and re-layouts  12.4 us (10%)
    pallas_call x4, Pallas kernels, run(): pl.pallas_call(kernel, out_shape=outs, in_specs=specs, out_specs=out_spec...  39.2 us
    ppermute x6, waiting for transfers between devices, swapped(): return lax.ppermute(value, 'chain', [(i, i ^ 1) for i in range(chain)])  25.8 us
    ppermute x6, starting transfers between devices, swapped(): return lax.ppermute(value, 'chain', [(i, i ^ 1) for i in range(chain)])  24.3 us
    ppermute x2, waiting for transfers between devices, onward(): return lax.ppermute(value, ('chain', 'group'), pairs)  12.7 us
    dynamic_slice x4, local copies, waits for them, and re-layouts, window(): return lax.dynamic_slice_in_dim(array, start, size, 0)  8.5 us
    unnamed x16, local copies, waits for them, and re-layouts  3.27 us
  transfers between devices with their start and end apart: 8, of which 3 were waited for; matrix products, arithmetic and copies ran while one was open for 8% of the time, Pallas kernels for 31%

profile of v2, /device:TPU:1, one launch (start us, length us, event | category | flops | bytes accessed | tf_op | source)
XLA Modules:
  0.0 119.5 jit_solution(15076512949104456965)
XLA Ops:
  0.0 0.0 copy-start.7
  0.0 0.0 copy-start.3
  0.0 0.7 copy-done.3
  0.7 0.0 copy-start.4
  0.7 0.7 copy-done.4
  1.4 0.0 copy-start.5
  1.4 0.7 copy-done.5
  2.0 2.9 %shard_map.73 = (bf16[4,1024,128]{2,1,0:T(8,128)(2,1)}, bf16[1,1024,128]{2,1,0:T(8,128)(2,1)S(1)}, f32[24,256]{1,0:T(8,128)S(1)}) custom-call(s32[1]{0:T(128)} %bitcast.1.role, s32[16]{0:T(128)S(1)} %bitcast.29, s32[16]{0:T(128)S(1)} %bitcast.30, f32[16,256]{1,0:T(8,128)S(1)} %bitcast.28, bf16[16,1024,128]{2,1,0:T(8,128)(2,1)} %bitcast.31), custom_call_target="tpu_custom_call" | custom-call | flops 1000000000 | bytes 8000000 | tf_op jit(solution)/shard_map/pallas_call | solution.py:367
  4.9 2.5 %collective-permute-start = (f32[24,256]{1,0:T(8,128)S(1)}, f32[24,256]{1,0:T(8,128)S(1)}, u32[]{:S(2)}, u32[]{:S(2)}) collective-permute-start(f32[24,256]{1,0:T(8,128)S(1)} %get-tuple-element.18), channel_id=1, source_target_pairs={{0,4},{4,0},{8,12},{12,8},{16,20},{20,16},{24,28},{28,24},{32,36},... | collective-permute-start | bytes 73736 | tf_op jit(solution)/shard_map/ppermute | solution.py:540
  7.5 0.1 collective-permute-start.4
  7.6 1.4 %collective-permute-start.5 = (bf16[1,1024,128]{2,1,0:T(8,128)(2,1)S(1)}, bf16[1,1024,128]{2,1,0:T(8,128)(2,1)S(1)}, u32[]{:S(2)}, u32[]{:S(2)}) collective-permute-start(bf16[1,1024,128]{2,1,0:T(8,128)(2,1)S(1)} %get-tuple-element.21), channel_id=1, source_target_pairs={{0,4},{4,0},{8,12},{12,8},{16,20},{20,16},{24,28},{28,24},{32,36},... | collective-permute-start | bytes 786440 | tf_op jit(solution)/shard_map/ppermute | solution.py:540
  8.9 2.1 %constant_dynamic-slice_fusion.3 = bf16[3,1024,128]{2,1,0:T(8,128)(2,1)} fusion(bf16[16,1024,128]{2,1,0:T(8,128)(2,1)} %bitcast.32, s32[]{:T(128)} %mul.14), kind=kLoop, calls=%fused_computation.11 | loop fusion | bytes 1572868 | tf_op jit(solution)/shard_map/dynamic_slice | solution.py:554
  11.0 0.1 collective-permute-start.1
  11.1 0.0 copy-done.7
  11.1 0.6 slice.20
  11.7 2.3 %constant_dynamic-slice_fusion.4.own = bf16[4,1024,128]{2,1,0:T(8,128)(2,1)} fusion(bf16[16,1024,128]{2,1,0:T(8,128)(2,1)} %bitcast.33, s32[]{:T(128)S(6)} %select_n.54), kind=kLoop, calls=%fused_computation.12 | loop fusion | bytes 2097156 | tf_op jit(solution)/shard_map/dynamic_slice | solution.py:554
  14.0 0.0 copy-start.6
  14.0 0.1 pad_add_fusion.1.role
  14.1 0.1 pad_add_fusion.role
  14.1 2.7 %constant_dynamic-slice_fusion = (bf16[4,512,256]{2,1,0:T(8,128)(2,1)}, bf16[4,512,256]{2,1,0:T(8,128)(2,1)S(1)}) fusion(bf16[16,512,256]{2,1,0:T(8,128)(2,1)} %param.11, s32[]{:T(128)S(6)} %select_n.63, s32[]{:T(128)S(6)} %select_n.61), kind=kLoop, calls=%fused_computation.8 | loop fusion | bytes 4194312 | tf_op jit(solution)/shard_map/dynamic_slice | solution.py:554
  16.8 1.5 %constant_dynamic-slice_fusion.1.own = bf16[6,1024,128]{2,1,0:T(8,128)(2,1)S(1)} fusion(bf16[16,1024,128]{2,1,0:T(8,128)(2,1)} %bitcast.34, s32[]{:T(128)S(6)} %select_n.62), kind=kLoop, calls=%fused_computation.9 | loop fusion | bytes 3145732 | tf_op jit(solution)/shard_map/dynamic_slice | solution.py:554
  18.3 0.0 copy-done.6
  18.3 0.7 pad_maximum_fusion.gates
  19.0 0.0 collective-permute-done
  19.0 0.7 collective-permute-start.2
  19.7 1.3 %collective-permute-start.3 = (f32[16,256]{1,0:T(8,128)S(1)}, f32[16,256]{1,0:T(8,128)S(1)}, u32[]{:S(2)}, u32[]{:S(2)}) collective-permute-start(f32[16,256]{1,0:T(8,128)S(1)} %get-tuple-element.35), channel_id=1, source_target_pairs={{4,8},{12,16},{20,24},{28,32},{36,40},{44,48},{52,56},{60,64},{68,... | collective-permute-start | bytes 49160 | tf_op jit(solution)/shard_map/ppermute | solution.py:547
  21.0 0.0 collective-permute-done.2
  21.0 12.7 %collective-permute-done.3 = f32[16,256]{1,0:T(8,128)S(1)} collective-permute-done((f32[16,256]{1,0:T(8,128)S(1)}, f32[16,256]{1,0:T(8,128)S(1)}, u32[]{:S(2)}, u32[]{:S(2)}) %collective-permute-start.3) | collective-permute-done | bytes 16416 | tf_op jit(solution)/shard_map/ppermute | solution.py:547
  33.8 0.1 broadcast_in_dim.7.scale
  33.8 0.0 collective-permute-done.4.got
  33.8 0.0 copy-start
  33.9 1.2 %copy-done = bf16[4,512,256]{2,1,0:T(8,128)(2,1)S(1)} copy-done((bf16[4,512,256]{2,1,0:T(8,128)(2,1)S(1)}, bf16[4,512,256]{2,1,0:T(8,128)(2,1)}, u32[]{:S(2)}) %copy-start) | copy-done | bytes 1048600
  35.1 0.0 copy-start.1
  35.1 5.1 %shard_map.74 = (bf16[3,512,512]{2,1,0:T(8,128)(2,1)S(1)}, bf16[3,2,512,256]{3,2,1,0:T(8,128)(2,1)S(1)}, f32[3,256,256]{2,1,0:T(8,128)S(1)}, bf16[6,256,256]{2,1,0:T(8,128)(2,1)S(1)}) custom-call(s32[3]{0:T(128)S(1)} %pad_add_fusion.1.role, f32[5]{0:T(128)S(1)} %pad_maximum_fusion.gates, s32[16]{0:T(128)S(1)} %fusion.2.kept, ...), custom_call_target="tpu_custom_call" | custom-call | flops 10000000000 | bytes 8000000 | tf_op jit(solution)/shard_map/pallas_call | solution.py:367
  40.2 0.0 collective-permute-done.5.got
  40.2 0.0 copy-done.1
  40.2 0.0 copy-start.2
  40.2 13.7 %shard_map.75 = (bf16[4,1024,128]{2,1,0:T(8,128)(2,1)}, bf16[16,1024,128]{2,1,0:T(8,128)(2,1)}, bf16[5,256,256]{2,1,0:T(8,128)(2,1)S(1)}) custom-call(s32[3]{0:T(128)S(1)} %pad_add_fusion.1.role, f32[5]{0:T(128)S(1)} %pad_maximum_fusion.gates, s32[16]{0:T(128)S(1)} %fusion.2.kept, bf16[6,1024,128]{2,1,0:T(8,128)(2,1)S(1)} %constant_dynamic-slice_fusion.1.own, ...), custom_call_target="tpu_custom_call" | custom-call | flops 10000000000 | bytes 8000000 | tf_op jit(solution)/shard_map/pallas_call | solution.py:367
  53.9 20.1 %collective-permute-start.7 = (bf16[4,1024,128]{2,1,0:T(8,128)(2,1)}, bf16[4,1024,128]{2,1,0:T(8,128)(2,1)S(1)}, u32[]{:S(2)}, u32[]{:S(2)}) collective-permute-start(bf16[4,1024,128]{2,1,0:T(8,128)(2,1)} %get-tuple-element.28), channel_id=1, source_target_pairs={{0,4},{4,0},{8,12},{12,8},{16,20},{20,16},{24,28},{28,24},{32,36},... | collective-permute-start | bytes 3145736 | tf_op jit(solution)/shard_map/ppermute | solution.py:540
  74.0 0.0 collective-permute-done.1.got
  74.0 0.0 copy-done.2
  74.0 17.5 %shard_map.76 = (bf16[4,1024,128]{2,1,0:T(8,128)(2,1)}, bf16[16,1024,128]{2,1,0:T(8,128)(2,1)}, bf16[1024,128]{1,0:T(8,128)(2,1)S(1)}) custom-call(s32[3]{0:T(128)S(1)} %pad_add_fusion.role, f32[5]{0:T(128)S(1)} %pad_maximum_fusion.gates, s32[16]{0:T(128)S(1)} %fusion.2.kept, bf16[4,1024,128]{2,1,0:T(8,128)(2,1)S(1)} %copy-done.2, ...), custom_call_target="tpu_custom_call", output_to_operand_aliasing={{1}: (9, {})} | custom-call | flops 10000000000 | bytes 8000000 | tf_op jit(solution)/shard_map/pallas_call | solution.py:367
  91.5 0.1 collective-permute-start.6
  91.6 4.3 %collective-permute-done.7.block = bf16[4,1024,128]{2,1,0:T(8,128)(2,1)S(1)} collective-permute-done((bf16[4,1024,128]{2,1,0:T(8,128)(2,1)}, bf16[4,1024,128]{2,1,0:T(8,128)(2,1)S(1)}, u32[]{:S(2)}, u32[]{:S(2)}) %collective-permute-start.7) | collective-permute-done | bytes 1048608 | tf_op jit(solution)/shard_map/ppermute | solution.py:540
  95.9 1.0 place.2.refs_0_
  96.9 21.5 %collective-permute-done.6.block = bf16[4,1024,128]{2,1,0:T(8,128)(2,1)S(1)} collective-permute-done((bf16[4,1024,128]{2,1,0:T(8,128)(2,1)}, bf16[4,1024,128]{2,1,0:T(8,128)(2,1)S(1)}, u32[]{:S(2)}, u32[]{:S(2)}) %collective-permute-start.6) | collective-permute-done | bytes 1048608 | tf_op jit(solution)/shard_map/ppermute | solution.py:540
  118.4 1.0 place.3
  (5 shorter events, 0.0 us)
Async XLA Ops:
  0.0 11.1 %copy-start.7 = (f32[3]{0:T(128)S(1)}, f32[3]{0:T(128)}, u32[]{:S(2)}) copy-start(f32[3]{0:T(128)} %param.13) | copy-start | bytes 40
  0.0 0.7 copy-start.3
  0.7 0.7 copy-start.4
  1.4 0.7 copy-start.5
  4.9 14.1 %collective-permute-start = (f32[24,256]{1,0:T(8,128)S(1)}, f32[24,256]{1,0:T(8,128)S(1)}, u32[]{:S(2)}, u32[]{:S(2)}) collective-permute-start(f32[24,256]{1,0:T(8,128)S(1)} %get-tuple-element.18), channel_id=1, source_target_pairs={{0,4},{4,0},{8,12},{12,8},{16,20},{20,16},{24,28},{28,24},{32,36},... | collective-permute-start | bytes 73736 | tf_op jit(solution)/shard_map/ppermute | solution.py:540
  7.5 26.4 %collective-permute-start.4 = (bf16[4,1024,128]{2,1,0:T(8,128)(2,1)}, bf16[4,1024,128]{2,1,0:T(8,128)(2,1)}, u32[]{:S(2)}, u32[]{:S(2)}) collective-permute-start(bf16[4,1024,128]{2,1,0:T(8,128)(2,1)} %get-tuple-element.19), channel_id=1, source_target_pairs={{0,4},{4,0},{8,12},{12,8},{16,20},{20,16},{24,28},{28,24},{32,36},... | collective-permute-start | bytes 3145736 | tf_op jit(solution)/shard_map/ppermute | solution.py:540
  7.6 32.6 %collective-permute-start.5 = (bf16[1,1024,128]{2,1,0:T(8,128)(2,1)S(1)}, bf16[1,1024,128]{2,1,0:T(8,128)(2,1)S(1)}, u32[]{:S(2)}, u32[]{:S(2)}) collective-permute-start(bf16[1,1024,128]{2,1,0:T(8,128)(2,1)S(1)} %get-tuple-element.21), channel_id=1, source_target_pairs={{0,4},{4,0},{8,12},{12,8},{16,20},{20,16},{24,28},{28,24},{32,36},... | collective-permute-start | bytes 786440 | tf_op jit(solution)/shard_map/ppermute | solution.py:540
  11.0 63.0 %collective-permute-start.1 = (bf16[3,1024,128]{2,1,0:T(8,128)(2,1)}, bf16[3,1024,128]{2,1,0:T(8,128)(2,1)}, u32[]{:S(2)}, u32[]{:S(2)}) collective-permute-start(bf16[3,1024,128]{2,1,0:T(8,128)(2,1)} %constant_dynamic-slice_fusion.3), channel_id=1, source_target_pairs={{0,4},{4,0},{8,12},{12,8},{16,20},{20,16},{24,28},{28,24},{32,36},... | collective-permute-start | bytes 2359304 | tf_op jit(solution)/shard_map/ppermute | solution.py:540
  14.0 4.3 %copy-start.6 = (f32[2]{0:T(128)S(1)}, f32[2]{0:T(128)}, u32[]{:S(2)}) copy-start(f32[2]{0:T(128)} %param.12) | copy-start | bytes 28
  19.0 2.0 %collective-permute-start.2 = (f32[16,256]{1,0:T(8,128)S(1)}, f32[16,256]{1,0:T(8,128)S(1)}, u32[]{:S(2)}, u32[]{:S(2)}) collective-permute-start(f32[16,256]{1,0:T(8,128)S(1)} %get-tuple-element.35), channel_id=1, source_target_pairs={{4,12},{12,20},{20,28},{28,36},{36,44},{44,52},{52,60},{60,68},{68... | collective-permute-start | bytes 49160 | tf_op jit(solution)/shard_map/ppermute | solution.py:547
  19.7 14.0 %collective-permute-start.3 = (f32[16,256]{1,0:T(8,128)S(1)}, f32[16,256]{1,0:T(8,128)S(1)}, u32[]{:S(2)}, u32[]{:S(2)}) collective-permute-start(f32[16,256]{1,0:T(8,128)S(1)} %get-tuple-element.35), channel_id=1, source_target_pairs={{4,8},{12,16},{20,24},{28,32},{36,40},{44,48},{52,56},{60,64},{68,... | collective-permute-start | bytes 49160 | tf_op jit(solution)/shard_map/ppermute | solution.py:547
  33.8 1.2 %copy-start = (bf16[4,512,256]{2,1,0:T(8,128)(2,1)S(1)}, bf16[4,512,256]{2,1,0:T(8,128)(2,1)}, u32[]{:S(2)}) copy-start(bf16[4,512,256]{2,1,0:T(8,128)(2,1)} %get-tuple-element.31.sketch) | copy-start | bytes 3145732
  35.1 5.1 %copy-start.1 = (bf16[4,512,256]{2,1,0:T(8,128)(2,1)S(1)}, bf16[4,512,256]{2,1,0:T(8,128)(2,1)}, u32[]{:S(2)}) copy-start(bf16[4,512,256]{2,1,0:T(8,128)(2,1)} %get-tuple-element.31.sketch) | copy-start | bytes 3145732
  40.2 33.8 %copy-start.2 = (bf16[4,1024,128]{2,1,0:T(8,128)(2,1)S(1)}, bf16[4,1024,128]{2,1,0:T(8,128)(2,1)}, u32[]{:S(2)}) copy-start(bf16[4,1024,128]{2,1,0:T(8,128)(2,1)} %constant_dynamic-slice_fusion.4.own) | copy-start | bytes 3145732
  53.9 42.0 %collective-permute-start.7 = (bf16[4,1024,128]{2,1,0:T(8,128)(2,1)}, bf16[4,1024,128]{2,1,0:T(8,128)(2,1)S(1)}, u32[]{:S(2)}, u32[]{:S(2)}) collective-permute-start(bf16[4,1024,128]{2,1,0:T(8,128)(2,1)} %get-tuple-element.28), channel_id=1, source_target_pairs={{0,4},{4,0},{8,12},{12,8},{16,20},{20,16},{24,28},{28,24},{32,36},... | collective-permute-start | bytes 3145736 | tf_op jit(solution)/shard_map/ppermute | solution.py:540
  91.5 26.9 %collective-permute-start.6 = (bf16[4,1024,128]{2,1,0:T(8,128)(2,1)}, bf16[4,1024,128]{2,1,0:T(8,128)(2,1)S(1)}, u32[]{:S(2)}, u32[]{:S(2)}) collective-permute-start(bf16[4,1024,128]{2,1,0:T(8,128)(2,1)} %get-tuple-element.27), channel_id=1, source_target_pairs={{0,4},{4,0},{8,12},{12,8},{16,20},{20,16},{24,28},{28,24},{32,36},... | collective-permute-start | bytes 3145736 | tf_op jit(solution)/shard_map/ppermute | solution.py:540
